TPU v7x, 32 devices: a 4x4x1 block of a 4x4x8 slice. The times are simulated.
32 devices in a mesh: dp: 1 (over z), tp: 32 (over y, x, core).
Axes of the slice: x: 4, y: 4, z: 1, core: 2. Of those that a mesh axis runs over, the one named last changes fastest.
The devices are a block of a 4x4x8 slice.
Arguments:
- x_in: bfloat16 [2048, 4096], P('dp')
- g_norm: bfloat16 [4096], replicated
- w_q: bfloat16 [4096, 4096], P(None, 'tp')
- w_k: bfloat16 [4096, 1024], replicated
- w_v: bfloat16 [4096, 1024], replicated
- w_o: bfloat16 [4096, 4096], P('tp')
- w_gate: bfloat16 [4096, 14336], P(None, 'tp')
- w_up: bfloat16 [4096, 14336], P(None, 'tp')
- w_down: bfloat16 [14336, 4096], P('tp')
Outputs:
- output 1: bfloat16 [2048, 4096], P('dp')
- output 2: bfloat16 [2048, 32, 128], P('dp', 'tp')
- output 3: bfloat16 [2048, 32, 128], P('dp', 'tp')
All inputs are finite; a program needn't handle non-finite values.
Results may differ from a plain program's by a relative error of at most 0.0147537.
Values are sent between devices in bfloat16 or wider.
A program may use at most 768 MiB of HBM per device.

v0:
```python
import math
import jax
import jax.numpy as jnp
from jax import lax
from jax.sharding import PartitionSpec as P

HEAD_DIM = 128
ROPE_BASE = 500000.0
NORM_EPS = 1e-5


def rope_tables(positions):
    inv_freq = ROPE_BASE ** (-jnp.arange(0, HEAD_DIM, 2, dtype=jnp.float32) / HEAD_DIM)
    angles = positions.astype(jnp.float32)[:, None] * inv_freq[None, :]
    return jnp.cos(angles), jnp.sin(angles)


def apply_rope(projected, cos_tab, sin_tab):
    half_dim = HEAD_DIM // 2
    lower_half = projected[..., :half_dim]
    upper_half = projected[..., half_dim:]
    cos_b = cos_tab[:, None, :]
    sin_b = sin_tab[:, None, :]
    return jnp.concatenate([lower_half * cos_b - upper_half * sin_b, upper_half * cos_b + lower_half * sin_b], axis=-1)


def rms_norm(x_rows, g_norm):
    x_f32 = x_rows.astype(jnp.float32)
    inv_rms = lax.rsqrt(jnp.mean(x_f32 * x_f32, axis=-1, keepdims=True) + NORM_EPS)
    return (x_f32 * inv_rms * g_norm.astype(jnp.float32)).astype(jnp.bfloat16)


def solution(mesh):
    tp_size = mesh.shape['tp']

    def local_layer(x_in, g_norm, w_q, w_k, w_v, w_o, w_gate, w_up, w_down):
        tokens, width = x_in.shape
        kv_heads = w_k.shape[1] // HEAD_DIM
        kv_local = max(kv_heads // tp_size, 1)
        q_local = w_q.shape[1] // HEAD_DIM
        group_size = q_local // kv_local
        q_block = min(128, tokens)
        score_scale = 1.0 / math.sqrt(HEAD_DIM)
        head_start = lax.axis_index('tp') * kv_heads // tp_size
        normed = rms_norm(x_in, g_norm)
        cos_tab, sin_tab = rope_tables(jnp.arange(tokens))
        w_k_mine = lax.dynamic_slice_in_dim(w_k, head_start * HEAD_DIM, kv_local * HEAD_DIM, axis=1)
        w_v_mine = lax.dynamic_slice_in_dim(w_v, head_start * HEAD_DIM, kv_local * HEAD_DIM, axis=1)
        k_proj = jnp.dot(normed, w_k_mine, preferred_element_type=jnp.float32).reshape(tokens, kv_local, HEAD_DIM)
        k_rot = apply_rope(k_proj, cos_tab, sin_tab).astype(jnp.bfloat16)
        v_proj = jnp.dot(normed, w_v_mine, preferred_element_type=jnp.float32).astype(jnp.bfloat16).reshape(tokens, kv_local, HEAD_DIM)
        key_pos = jnp.arange(tokens)

        def row_block(block_idx):
            row_start = block_idx * q_block
            normed_blk = lax.dynamic_slice_in_dim(normed, row_start, q_block, axis=0)
            cos_blk = lax.dynamic_slice_in_dim(cos_tab, row_start, q_block, axis=0)
            sin_blk = lax.dynamic_slice_in_dim(sin_tab, row_start, q_block, axis=0)
            q_proj = jnp.dot(normed_blk, w_q, preferred_element_type=jnp.float32).reshape(q_block, q_local, HEAD_DIM)
            q_rot = apply_rope(q_proj, cos_blk, sin_blk).astype(jnp.bfloat16).reshape(q_block, kv_local, group_size, HEAD_DIM)
            scores = jnp.einsum('qgrd,kgd->grqk', q_rot, k_rot, preferred_element_type=jnp.float32) * score_scale
            query_pos = row_start + jnp.arange(q_block)
            scores = jnp.where(key_pos[None, :] <= query_pos[:, None], scores, -1e30)
            probs_bf = jax.nn.softmax(scores, axis=-1).astype(jnp.bfloat16)
            attn_out = jnp.einsum('grqk,kgd->qgrd', probs_bf, v_proj, preferred_element_type=jnp.float32).astype(jnp.bfloat16).reshape(q_block, q_local * HEAD_DIM)
            gate_proj = jnp.dot(normed_blk, w_gate, preferred_element_type=jnp.float32)
            up_proj = jnp.dot(normed_blk, w_up, preferred_element_type=jnp.float32)
            hidden = (jax.nn.silu(gate_proj) * up_proj).astype(jnp.bfloat16)
            return (jnp.dot(attn_out, w_o, preferred_element_type=jnp.float32) + jnp.dot(hidden, w_down, preferred_element_type=jnp.float32)).astype(jnp.bfloat16)

        partial_sum = lax.map(row_block, jnp.arange(tokens // q_block)).reshape(tokens, width)
        reduced_sum = lax.psum(partial_sum, 'tp')
        y_out = (x_in.astype(jnp.float32) + reduced_sum.astype(jnp.float32)).astype(jnp.bfloat16)
        return y_out, k_rot, v_proj

    return jax.shard_map(local_layer, mesh=mesh, in_specs=(P('dp', None), P(None), P(None, 'tp'), P(None, None), P(None, None), P('tp', None), P(None, 'tp'), P(None, 'tp'), P('tp', None)), out_specs=(P('dp', None), P('dp', 'tp', None), P('dp', 'tp', None)), check_vma=False)
```

profile of v0, /device:TPU:97, one launch (start us, length us, event | category | flops | bytes accessed | tf_op | source)
XLA Modules:
  0.0 559.2 jit_solution(6866331131341350356)
XLA Ops:
  7.3 7.2 %fusion.43 = f32[2048]{0:T(1024)S(1)} fusion(bf16[2048,4096]{1,0:T(8,128)(2,1)} %param.11), kind=kLoop, calls=%fused_computation.53 | loop fusion | flops 25163776 | bytes 16785408 | tf_op jit(solution)/shard_map/reduce_sum | solution.py:29
  14.6 15.5 %fusion.45 = bf16[2048,4096]{1,0:T(8,128)(2,1)} fusion(bf16[2048,4096]{1,0:T(8,128)(2,1)} %param.11, f32[4096]{0:T(1024)S(1)} %convert_element_type.72, f32[2048]{0:T(1024)S(1)} %add_rsqrt_fusion), kind=kLoop, calls=%fused_computation.55 | loop fusion | flops 33554432 | bytes 33579008 | tf_op jit(solution)/shard_map/convert_element_type | solution.py:30
  30.1 2.8 multiply_sine_fusion.1
  32.9 11.7 %convolution_bitcast_fusion.1 = f32[2048,1,128]{0,2,1:T(8,128)S(1)} fusion(bf16[2048,4096]{1,0:T(8,128)(2,1)} %fusion.45, bf16[4096,1024]{1,0:T(8,128)(2,1)} %param.14, s32[]{:T(128)S(6)} %select_n.19), kind=kOutput, calls=%fused_computation.57 | convolution fusion | flops 2147483648 | bytes 18874372 | tf_op jit(solution)/shard_map/dot_general | solution.py:49
  44.5 2.3 fusion.55
  47.9 11.3 %fusion.47 = bf16[2048,1,128]{2,0,1:T(8,128)(2,1)} fusion(bf16[2048,4096]{1,0:T(8,128)(2,1)} %fusion.45, bf16[4096,1024]{1,0:T(8,128)(2,1)} %param.15, s32[]{:T(128)S(6)} %select_n.19), kind=kOutput, calls=%fused_computation.59 | convolution fusion | flops 2147745792 | bytes 18350084 | tf_op jit(solution)/shard_map/dot_general | solution.py:51
  59.2 303.3 %while.11 = (s32[]{:T(128)}, bf16[16,128,4096]{2,1,0:T(8,128)(2,1)}, s32[16]{0:T(128)S(1)}, bf16[2048,4096]{1,0:T(8,128)(2,1)}, bf16[4096,128]{1,0:T(8,128)(2,1)...) while((s32[]{:T(128)}, ...), condition=%wide.region_4.5_spmd.clone, body=%wide.region_1.4_spmd.clone.sunk | while | flops 1815838592 | bytes 26415340 | solution.py:71
  60.5 2.1 convolution_bitcast_fusion.3
  65.2 2.2 fusion.97
  67.4 3.5 fusion.98
  70.9 7.3 %fusion.99 = bf16[16,128,4096]{2,1,0:T(8,128)(2,1)} fusion(bf16[16,128,4096]{2,1,0:T(8,128)(2,1)} %get-tuple-element.275, s32[]{:T(128)} %get-tuple-element.274, f32[128,4096]{1,0:T(8,128)S(1)} %fusion.97, bf16[448,4096]{1,0:T(8,128)(2,1)} %get-tuple-element.303, bf16[4096,448]{0,1:T(8,128)(2,1)} %get-tuple-element.302, ...), kind=kOutput, calls=%fused_computation.4.clone.1 | convolution fusion | flops 940916736 | bytes 11764228 | tf_op jit(solution)/shard_map/while/body/eval_jaxpr/dot_general | solution.py:69
  79.5 2.1 convolution_bitcast_fusion.3
  84.2 2.2 fusion.97
  86.3 3.5 fusion.98
  89.8 7.3 %fusion.99 = bf16[16,128,4096]{2,1,0:T(8,128)(2,1)} fusion(bf16[16,128,4096]{2,1,0:T(8,128)(2,1)} %get-tuple-element.275, s32[]{:T(128)} %get-tuple-element.274, f32[128,4096]{1,0:T(8,128)S(1)} %fusion.97, bf16[448,4096]{1,0:T(8,128)(2,1)} %get-tuple-element.303, bf16[4096,448]{0,1:T(8,128)(2,1)} %get-tuple-element.302, ...), kind=kOutput, calls=%fused_computation.4.clone.1 | convolution fusion | flops 940916736 | bytes 11764228 | tf_op jit(solution)/shard_map/while/body/eval_jaxpr/dot_general | solution.py:69
  98.5 2.1 convolution_bitcast_fusion.3
  103.1 2.2 fusion.97
  105.3 3.5 fusion.98
  108.8 7.3 %fusion.99 = bf16[16,128,4096]{2,1,0:T(8,128)(2,1)} fusion(bf16[16,128,4096]{2,1,0:T(8,128)(2,1)} %get-tuple-element.275, s32[]{:T(128)} %get-tuple-element.274, f32[128,4096]{1,0:T(8,128)S(1)} %fusion.97, bf16[448,4096]{1,0:T(8,128)(2,1)} %get-tuple-element.303, bf16[4096,448]{0,1:T(8,128)(2,1)} %get-tuple-element.302, ...), kind=kOutput, calls=%fused_computation.4.clone.1 | convolution fusion | flops 940916736 | bytes 11764228 | tf_op jit(solution)/shard_map/while/body/eval_jaxpr/dot_general | solution.py:69
  117.4 2.1 convolution_bitcast_fusion.3
  122.1 2.2 fusion.97
  124.3 3.5 fusion.98
  127.7 7.3 %fusion.99 = bf16[16,128,4096]{2,1,0:T(8,128)(2,1)} fusion(bf16[16,128,4096]{2,1,0:T(8,128)(2,1)} %get-tuple-element.275, s32[]{:T(128)} %get-tuple-element.274, f32[128,4096]{1,0:T(8,128)S(1)} %fusion.97, bf16[448,4096]{1,0:T(8,128)(2,1)} %get-tuple-element.303, bf16[4096,448]{0,1:T(8,128)(2,1)} %get-tuple-element.302, ...), kind=kOutput, calls=%fused_computation.4.clone.1 | convolution fusion | flops 940916736 | bytes 11764228 | tf_op jit(solution)/shard_map/while/body/eval_jaxpr/dot_general | solution.py:69
  141.0 2.2 fusion.97
  143.2 3.5 fusion.98
  146.7 7.3 %fusion.99 = bf16[16,128,4096]{2,1,0:T(8,128)(2,1)} fusion(bf16[16,128,4096]{2,1,0:T(8,128)(2,1)} %get-tuple-element.275, s32[]{:T(128)} %get-tuple-element.274, f32[128,4096]{1,0:T(8,128)S(1)} %fusion.97, bf16[448,4096]{1,0:T(8,128)(2,1)} %get-tuple-element.303, bf16[4096,448]{0,1:T(8,128)(2,1)} %get-tuple-element.302, ...), kind=kOutput, calls=%fused_computation.4.clone.1 | convolution fusion | flops 940916736 | bytes 11764228 | tf_op jit(solution)/shard_map/while/body/eval_jaxpr/dot_general | solution.py:69
  160.0 2.2 fusion.97
  162.2 3.5 fusion.98
  165.6 7.3 %fusion.99 = bf16[16,128,4096]{2,1,0:T(8,128)(2,1)} fusion(bf16[16,128,4096]{2,1,0:T(8,128)(2,1)} %get-tuple-element.275, s32[]{:T(128)} %get-tuple-element.274, f32[128,4096]{1,0:T(8,128)S(1)} %fusion.97, bf16[448,4096]{1,0:T(8,128)(2,1)} %get-tuple-element.303, bf16[4096,448]{0,1:T(8,128)(2,1)} %get-tuple-element.302, ...), kind=kOutput, calls=%fused_computation.4.clone.1 | convolution fusion | flops 940916736 | bytes 11764228 | tf_op jit(solution)/shard_map/while/body/eval_jaxpr/dot_general | solution.py:69
  178.9 2.2 fusion.97
  181.1 3.5 fusion.98
  184.6 7.3 %fusion.99 = bf16[16,128,4096]{2,1,0:T(8,128)(2,1)} fusion(bf16[16,128,4096]{2,1,0:T(8,128)(2,1)} %get-tuple-element.275, s32[]{:T(128)} %get-tuple-element.274, f32[128,4096]{1,0:T(8,128)S(1)} %fusion.97, bf16[448,4096]{1,0:T(8,128)(2,1)} %get-tuple-element.303, bf16[4096,448]{0,1:T(8,128)(2,1)} %get-tuple-element.302, ...), kind=kOutput, calls=%fused_computation.4.clone.1 | convolution fusion | flops 940916736 | bytes 11764228 | tf_op jit(solution)/shard_map/while/body/eval_jaxpr/dot_general | solution.py:69
  197.9 2.2 fusion.97
  200.1 3.5 fusion.98
  203.6 7.3 %fusion.99 = bf16[16,128,4096]{2,1,0:T(8,128)(2,1)} fusion(bf16[16,128,4096]{2,1,0:T(8,128)(2,1)} %get-tuple-element.275, s32[]{:T(128)} %get-tuple-element.274, f32[128,4096]{1,0:T(8,128)S(1)} %fusion.97, bf16[448,4096]{1,0:T(8,128)(2,1)} %get-tuple-element.303, bf16[4096,448]{0,1:T(8,128)(2,1)} %get-tuple-element.302, ...), kind=kOutput, calls=%fused_computation.4.clone.1 | convolution fusion | flops 940916736 | bytes 11764228 | tf_op jit(solution)/shard_map/while/body/eval_jaxpr/dot_general | solution.py:69
  216.9 2.2 fusion.97
  219.0 3.5 fusion.98
  222.5 7.3 %fusion.99 = bf16[16,128,4096]{2,1,0:T(8,128)(2,1)} fusion(bf16[16,128,4096]{2,1,0:T(8,128)(2,1)} %get-tuple-element.275, s32[]{:T(128)} %get-tuple-element.274, f32[128,4096]{1,0:T(8,128)S(1)} %fusion.97, bf16[448,4096]{1,0:T(8,128)(2,1)} %get-tuple-element.303, bf16[4096,448]{0,1:T(8,128)(2,1)} %get-tuple-element.302, ...), kind=kOutput, calls=%fused_computation.4.clone.1 | convolution fusion | flops 940916736 | bytes 11764228 | tf_op jit(solution)/shard_map/while/body/eval_jaxpr/dot_general | solution.py:69
  235.8 2.2 fusion.97
  238.0 3.5 fusion.98
  241.5 7.3 %fusion.99 = bf16[16,128,4096]{2,1,0:T(8,128)(2,1)} fusion(bf16[16,128,4096]{2,1,0:T(8,128)(2,1)} %get-tuple-element.275, s32[]{:T(128)} %get-tuple-element.274, f32[128,4096]{1,0:T(8,128)S(1)} %fusion.97, bf16[448,4096]{1,0:T(8,128)(2,1)} %get-tuple-element.303, bf16[4096,448]{0,1:T(8,128)(2,1)} %get-tuple-element.302, ...), kind=kOutput, calls=%fused_computation.4.clone.1 | convolution fusion | flops 940916736 | bytes 11764228 | tf_op jit(solution)/shard_map/while/body/eval_jaxpr/dot_general | solution.py:69
  254.8 2.2 fusion.97
  256.9 3.5 fusion.98
  260.4 7.3 %fusion.99 = bf16[16,128,4096]{2,1,0:T(8,128)(2,1)} fusion(bf16[16,128,4096]{2,1,0:T(8,128)(2,1)} %get-tuple-element.275, s32[]{:T(128)} %get-tuple-element.274, f32[128,4096]{1,0:T(8,128)S(1)} %fusion.97, bf16[448,4096]{1,0:T(8,128)(2,1)} %get-tuple-element.303, bf16[4096,448]{0,1:T(8,128)(2,1)} %get-tuple-element.302, ...), kind=kOutput, calls=%fused_computation.4.clone.1 | convolution fusion | flops 940916736 | bytes 11764228 | tf_op jit(solution)/shard_map/while/body/eval_jaxpr/dot_general | solution.py:69
  269.1 2.1 convolution_bitcast_fusion.3
  273.7 2.2 fusion.97
  275.9 3.5 fusion.98
  279.4 7.3 %fusion.99 = bf16[16,128,4096]{2,1,0:T(8,128)(2,1)} fusion(bf16[16,128,4096]{2,1,0:T(8,128)(2,1)} %get-tuple-element.275, s32[]{:T(128)} %get-tuple-element.274, f32[128,4096]{1,0:T(8,128)S(1)} %fusion.97, bf16[448,4096]{1,0:T(8,128)(2,1)} %get-tuple-element.303, bf16[4096,448]{0,1:T(8,128)(2,1)} %get-tuple-element.302, ...), kind=kOutput, calls=%fused_computation.4.clone.1 | convolution fusion | flops 940916736 | bytes 11764228 | tf_op jit(solution)/shard_map/while/body/eval_jaxpr/dot_general | solution.py:69
  292.7 2.2 fusion.97
  294.9 3.5 fusion.98
  298.3 7.3 %fusion.99 = bf16[16,128,4096]{2,1,0:T(8,128)(2,1)} fusion(bf16[16,128,4096]{2,1,0:T(8,128)(2,1)} %get-tuple-element.275, s32[]{:T(128)} %get-tuple-element.274, f32[128,4096]{1,0:T(8,128)S(1)} %fusion.97, bf16[448,4096]{1,0:T(8,128)(2,1)} %get-tuple-element.303, bf16[4096,448]{0,1:T(8,128)(2,1)} %get-tuple-element.302, ...), kind=kOutput, calls=%fused_computation.4.clone.1 | convolution fusion | flops 940916736 | bytes 11764228 | tf_op jit(solution)/shard_map/while/body/eval_jaxpr/dot_general | solution.py:69
  307.0 2.1 convolution_bitcast_fusion.3
  311.6 2.2 fusion.97
  313.8 3.5 fusion.98
  317.3 7.3 %fusion.99 = bf16[16,128,4096]{2,1,0:T(8,128)(2,1)} fusion(bf16[16,128,4096]{2,1,0:T(8,128)(2,1)} %get-tuple-element.275, s32[]{:T(128)} %get-tuple-element.274, f32[128,4096]{1,0:T(8,128)S(1)} %fusion.97, bf16[448,4096]{1,0:T(8,128)(2,1)} %get-tuple-element.303, bf16[4096,448]{0,1:T(8,128)(2,1)} %get-tuple-element.302, ...), kind=kOutput, calls=%fused_computation.4.clone.1 | convolution fusion | flops 940916736 | bytes 11764228 | tf_op jit(solution)/shard_map/while/body/eval_jaxpr/dot_general | solution.py:69
  330.6 2.2 fusion.97
  332.8 3.5 fusion.98
  336.3 7.3 %fusion.99 = bf16[16,128,4096]{2,1,0:T(8,128)(2,1)} fusion(bf16[16,128,4096]{2,1,0:T(8,128)(2,1)} %get-tuple-element.275, s32[]{:T(128)} %get-tuple-element.274, f32[128,4096]{1,0:T(8,128)S(1)} %fusion.97, bf16[448,4096]{1,0:T(8,128)(2,1)} %get-tuple-element.303, bf16[4096,448]{0,1:T(8,128)(2,1)} %get-tuple-element.302, ...), kind=kOutput, calls=%fused_computation.4.clone.1 | convolution fusion | flops 940916736 | bytes 11764228 | tf_op jit(solution)/shard_map/while/body/eval_jaxpr/dot_general | solution.py:69
  344.9 2.1 convolution_bitcast_fusion.3
  349.5 2.2 fusion.97
  351.7 3.5 fusion.98
  355.2 7.3 %fusion.99 = bf16[16,128,4096]{2,1,0:T(8,128)(2,1)} fusion(bf16[16,128,4096]{2,1,0:T(8,128)(2,1)} %get-tuple-element.275, s32[]{:T(128)} %get-tuple-element.274, f32[128,4096]{1,0:T(8,128)S(1)} %fusion.97, bf16[448,4096]{1,0:T(8,128)(2,1)} %get-tuple-element.303, bf16[4096,448]{0,1:T(8,128)(2,1)} %get-tuple-element.302, ...), kind=kOutput, calls=%fused_computation.4.clone.1 | convolution fusion | flops 940916736 | bytes 11764228 | tf_op jit(solution)/shard_map/while/body/eval_jaxpr/dot_general | solution.py:69
  362.5 170.4 %all-reduce.2.cloned.1.call-done = bf16[2048,4096]{1,0:T(8,128)(2,1)} async-done(((bf16[2048,4096]{1,0:T(8,128)(2,1)}), bf16[2048,4096]{1,0:T(8,128)(2,1)}) %all-reduce.2.cloned.1.call-update) | async-done | bytes 16777232 | tf_op jit(solution)/shard_map/psum | solution.py:72
  533.0 19.3 %fusion.46 = bf16[2048,4096]{1,0:T(8,128)(2,1)} fusion(bf16[2048,4096]{1,0:T(8,128)(2,1)} %param.11, bf16[2048,4096]{1,0:T(8,128)(2,1)} %all-reduce.2.cloned.1.call-done), kind=kLoop, calls=%fused_computation.56 | loop fusion | flops 33554432 | bytes 50331648 | tf_op jit(solution)/shard_map/convert_element_type | solution.py:73
  (101 shorter events, 71.5 us)
Async XLA Ops:
  7.2 7.4 %copy-start = (bf16[4096]{0:T(1024)(128)(2,1)S(1)}, bf16[4096]{0:T(1024)(128)(2,1)}, u32[]{:S(2)}) copy-start(bf16[4096]{0:T(1024)(128)(2,1)} %param.12) | copy-start | bytes 24580
  7.2 525.8 %all-reduce.2.cloned.1.call-start = ((), (), s32[]{:S(2)}) async-start(), calls=%async_computation | async-start | bytes 33554432 | tf_op jit(solution)/shard_map/psum | solution.py:72
Sparse Core Ops, SparseCore 0:
  362.7 170.2 all-reduce.1
where the time goes:
time: 563 us; the launch traced here: 559 us
  matrix products  286 us (51%)
  waiting for transfers between devices  171 us (30%)
  other arithmetic  64.9 us (12%)
  between operations  14.2 us (3%)
  loops' own time  11.7 us (2%)
  local copies, waits for them, and re-layouts  11.5 us (2%)
    psum x1, waiting for transfers between devices, local_layer(): reduced_sum = lax.psum(partial_sum, 'tp')  170 us
    dot_general x16, matrix products, row_block(): jnp.dot(hidden, w_down, preferred_element_type=jnp.float32)  116 us
    dot_general x16, matrix products, row_block(): gate_proj = jnp.dot(normed_blk, w_gate, preferred_element_type=jnp.float32)  55.6 us
    dot_general x16, matrix products, row_block(): jnp.dot(attn_out, w_o, preferred_element_type=jnp.float32)  34.8 us
    dot_general x16, matrix products, row_block(): jnp.dot(normed_blk, w_q, preferred_element_type=jnp.float32)  33 us
    dot_general x16, matrix products, row_block(): jnp.einsum('qgrd,kgd->grqk', q_rot, k_rot, preferred_element_type=jnp.flo...  23.5 us
    convert_element_type x1, other arithmetic, local_layer(): (x_in.astype(jnp.float32) + reduced_sum.astype(jnp.float32)).astype(jnp.b...  19.3 us
    convert_element_type x2, other arithmetic, rms_norm(): return (x_f32 * inv_rms * g_norm.astype(jnp.float32)).astype(jnp.bfloat16)  15.5 us
  transfers between devices with their start and end apart: 1, of which 1 were waited for; matrix products, arithmetic and copies ran while one was open for 0% of the time, Pallas kernels for 0%

commit v1 on v0

v1 whole, which is shorter than its diff:
```python
import functools
import math
import jax
import jax.numpy as jnp
from jax import lax
from jax.experimental import pallas as pl
from jax.experimental.pallas import tpu as pltpu
from jax.sharding import PartitionSpec as P

HEAD_DIM = 128
ROPE_BASE = 500000.0
NORM_EPS = 1e-5
LANES = 128
ROWS = 128
KEYS = 512
OUT_TILE = 1024
LAG = (0, 1, 2, 3, 4, 5, 6, 7, 8, 9, 10)
BF16 = jnp.bfloat16
F32 = jnp.float32


def layer_kernel(cfg, x_hbm, g_ref, cos_hbm, sin_hbm, wq_hbm, wk_hbm, wv_hbm, wo_hbm, wg_hbm, wu_hbm, wd_hbm,
                 y_hbm, k_hbm, v_hbm,
                 wqkv, wg, wu, wod, xbuf, tabs, abuf, ombuf, kbuf, vbuf, part, quart, r1, r2, r3, r4, xres, ybuf,
                 wsem, xsem, ressem, kvsem, ysem, pair_send, pair_recv, ssem, rsem, gpair_send, gpair_recv):
    tokens, width = x_hbm.shape
    tp, side, kv_heads = cfg
    nblk = tokens // ROWS
    half = width // 2
    quarter = half // 2
    cw = quarter // side
    ch = cw // 2
    rw = ROWS // side
    ff = wg.shape[1]

    me = lax.axis_index("tp")
    core = lax.rem(me, 2)
    px = lax.rem(me // 2, side)
    py = me // (2 * side)
    partner = me + 1 - 2 * core

    def wrap(p):
        return lax.rem(p + side, side)

    def at(y, x):
        return (wrap(y) * side + wrap(x)) * 2 + core

    near = (((at(py, px + 1)), (at(py, px - 1))), ((at(py + 1, px)), (at(py - 1, px))))
    pos = (px, py)

    def dev(d):
        return {"tp": d}

    barrier = pltpu.get_barrier_semaphore()
    for d in (partner, *near[0], *near[1]):
        pl.semaphore_signal(barrier, inc=1, device_id=dev(d), device_id_type=pl.DeviceIdType.MESH)

    head = lax.div(me * kv_heads, tp)
    kcol = pl.ds(pl.multiple_of(head * HEAD_DIM, HEAD_DIM), HEAD_DIM)
    mine0 = core * half
    res_col = [pl.multiple_of(mine0 + ab * quarter + pos[ab] * cw, cw) for ab in (0, 1)]

    def x_load(b, slot):
        rows = pl.ds(pl.multiple_of(b * ROWS, ROWS), ROWS)
        return (pltpu.make_async_copy(x_hbm.at[rows], xbuf.at[slot], xsem.at[slot, 0]),
                pltpu.make_async_copy(cos_hbm.at[rows], tabs.at[slot, 0], xsem.at[slot, 1]),
                pltpu.make_async_copy(sin_hbm.at[rows], tabs.at[slot, 1], xsem.at[slot, 2]))

    w_loads = (
        pltpu.make_async_copy(wq_hbm, wqkv.at[:, pl.ds(0, HEAD_DIM)], wsem.at[0]),
        pltpu.make_async_copy(wk_hbm.at[:, kcol], wqkv.at[:, pl.ds(HEAD_DIM, HEAD_DIM)], wsem.at[1]),
        pltpu.make_async_copy(wv_hbm.at[:, kcol], wqkv.at[:, pl.ds(2 * HEAD_DIM, HEAD_DIM)], wsem.at[2]),
        pltpu.make_async_copy(wg_hbm, wg, wsem.at[3]),
        pltpu.make_async_copy(wu_hbm, wu, wsem.at[4]),
        pltpu.make_async_copy(wo_hbm, wod.at[pl.ds(0, HEAD_DIM)], wsem.at[5]),
        pltpu.make_async_copy(wd_hbm, wod.at[pl.ds(HEAD_DIM, ff)], wsem.at[6]),
    )
    for c in x_load(0, 0):
        c.start()
    for c in w_loads:
        c.start()
    res_loads = [pltpu.make_async_copy(x_hbm.at[:, pl.ds(res_col[ab], cw)], xres.at[ab], ressem.at[ab]) for ab in (0, 1)]
    for c in res_loads:
        c.start()
    kbuf[...] = jnp.zeros_like(kbuf)
    vbuf[...] = jnp.zeros_like(vbuf)

    def pair_copy(b):
        col = pl.multiple_of((1 - core) * half, half)
        return pltpu.make_async_remote_copy(
            src_ref=part.at[lax.rem(b, 2), :, pl.ds(col, half)], dst_ref=quart.at[b],
            send_sem=pair_send.at[lax.rem(b, 2)], recv_sem=pair_recv.at[b],
            device_id=dev(partner), device_id_type=pl.DeviceIdType.MESH)

    def hop(src, dst, st, b, ab, d, axis):
        return pltpu.make_async_remote_copy(
            src_ref=src, dst_ref=dst, send_sem=ssem.at[st, ab, d, lax.rem(b, 2)], recv_sem=rsem.at[st, ab, d, b],
            device_id=dev(near[axis][d]), device_id_type=pl.DeviceIdType.MESH)

    def qcols(ab, chunk, h=None):
        base = ab * quarter + wrap(chunk) * cw
        if h is None:
            return pl.ds(pl.multiple_of(base, cw), cw)
        return pl.ds(pl.multiple_of(base + h * ch, ch), ch)

    def ycols(ab, chunk, h=None):
        base = mine0 + ab * quarter + wrap(chunk) * cw
        if h is None:
            return pl.ds(pl.multiple_of(base, cw), cw)
        return pl.ds(pl.multiple_of(base + h * ch, ch), ch)

    def brows(chunk):
        return pl.ds(pl.multiple_of(wrap(chunk) * rw, rw), rw)

    def yrows(b, chunk=None):
        if chunk is None:
            return pl.ds(pl.multiple_of(b * ROWS, ROWS), ROWS)
        return pl.ds(pl.multiple_of(b * ROWS + wrap(chunk) * rw, rw), rw)

    def send1(b, ab, d):
        p = pos[ab]
        return hop(quart.at[b, :, qcols(ab, p + 2, d)], r1.at[b, ab, d], 0, b, ab, d, ab)

    def send2(b, ab, d):
        p = pos[ab]
        return hop(quart.at[b, :, qcols(ab, p + 1 - 2 * d)], r2.at[b, ab, d], 1, b, ab, d, ab)

    def send3(b, ab, d):
        p2 = pos[1 - ab]
        return hop(quart.at[b, brows(p2 + 2), qcols(ab, pos[ab], d)], r3.at[b, ab, d], 2, b, ab, d, 1 - ab)

    def send4(b, ab, d):
        p2 = pos[1 - ab]
        return hop(quart.at[b, brows(p2 + 1 - 2 * d), qcols(ab, pos[ab])], r4.at[b, ab, d], 3, b, ab, d, 1 - ab)

    def y_hop(b, rows, cols, st, ab, d, axis):
        return hop(ybuf.at[rows, cols], ybuf.at[rows, cols], st, b, ab, d, axis)

    def send5(b, ab, d):
        return y_hop(b, yrows(b, pos[1 - ab]), ycols(ab, pos[ab]), 4, ab, d, 1 - ab)

    def land5(b, ab, d):
        return y_hop(b, yrows(b, pos[1 - ab] - 1 + 2 * d), ycols(ab, pos[ab]), 4, ab, d, 1 - ab)

    def send6(b, ab, d):
        return y_hop(b, yrows(b, pos[1 - ab] - 1 + 2 * d), ycols(ab, pos[ab], d), 5, ab, d, 1 - ab)

    def land6(b, ab, d):
        return y_hop(b, yrows(b, pos[1 - ab] + 2), ycols(ab, pos[ab], d), 5, ab, d, 1 - ab)

    def send7(b, ab, d):
        return y_hop(b, yrows(b), ycols(ab, pos[ab]), 6, ab, d, ab)

    def land7(b, ab, d):
        return y_hop(b, yrows(b), ycols(ab, pos[ab] - 1 + 2 * d), 6, ab, d, ab)

    def send8(b, ab, d):
        return y_hop(b, yrows(b), ycols(ab, pos[ab] - 1 + 2 * d, d), 7, ab, d, ab)

    def land8(b, ab, d):
        return y_hop(b, yrows(b), ycols(ab, pos[ab] + 2, d), 7, ab, d, ab)

    sends = (send1, send2, send3, send4, send5, send6, send7, send8)

    def gpair(b, c):
        cols = pl.ds(pl.multiple_of(c * half, half), half)
        return pltpu.make_async_remote_copy(
            src_ref=ybuf.at[yrows(b), cols], dst_ref=ybuf.at[yrows(b), cols],
            send_sem=gpair_send.at[lax.rem(b, 2)], recv_sem=gpair_recv.at[b],
            device_id=dev(partner), device_id_type=pl.DeviceIdType.MESH)

    def y_store(b):
        return pltpu.make_async_copy(ybuf.at[yrows(b)], y_hbm.at[yrows(b)], ysem.at[lax.rem(b, 2)])

    def kv_store(b):
        rows = yrows(b)
        slot = lax.rem(b, 2)
        return (pltpu.make_async_copy(kbuf.at[rows], k_hbm.at[rows], kvsem.at[slot, 0]),
                pltpu.make_async_copy(vbuf.at[rows], v_hbm.at[rows], kvsem.at[slot, 1]))

    def issue(send, b):
        for ab in (0, 1):
            for d in (0, 1):
                @pl.when(b >= 2)
                def _():
                    send(b - 2, ab, d).wait_send()
                send(b, ab, d).start()

    def attend(q, b, keys):
        ks = kbuf[pl.ds(0, keys), :]
        s = lax.dot_general(q, ks, (((1,), (1,)), ((), ())), preferred_element_type=F32)
        s = s * (1.0 / math.sqrt(HEAD_DIM))
        qpos = b * ROWS + lax.broadcasted_iota(jnp.int32, s.shape, 0)
        kpos = lax.broadcasted_iota(jnp.int32, s.shape, 1)
        s = jnp.where(kpos <= qpos, s, -1e30)
        top = jnp.max(s, axis=-1, keepdims=True)
        e = jnp.exp(s - top)
        probs = (e * (1.0 / jnp.sum(e, axis=-1, keepdims=True))).astype(BF16)
        o = jnp.dot(probs, vbuf[pl.ds(0, keys), :], preferred_element_type=F32)
        ombuf[:, pl.ds(0, HEAD_DIM)] = o.astype(BF16)

    def compute(b):
        slot = lax.rem(b, 2)
        for c in x_load(b, slot):
            c.wait()

        @pl.when(b + 1 < nblk)
        def _():
            for c in x_load(b + 1, 1 - slot):
                c.start()

        @pl.when(b == 0)
        def _():
            for c in w_loads[:3]:
                c.wait()

        for r in range(0, ROWS, 16):
            xr = xbuf[slot, pl.ds(r, 16), :].astype(F32)
            inv = lax.rsqrt(jnp.mean(xr * xr, axis=-1, keepdims=True) + NORM_EPS)
            abuf[pl.ds(r, 16), :] = (xr * inv * g_ref[...].astype(F32)).astype(BF16)

        a = abuf[...]
        qkv = jnp.dot(a, wqkv[...], preferred_element_type=F32)
        cos_t = tabs[slot, 0]
        sin_t = tabs[slot, 1]

        def rope(z):
            return (z * cos_t + pltpu.roll(z, HEAD_DIM // 2, 1) * sin_t).astype(BF16)

        q = rope(qkv[:, :HEAD_DIM])
        rows = yrows(b)
        kbuf[rows, :] = rope(qkv[:, HEAD_DIM:2 * HEAD_DIM])
        vbuf[rows, :] = qkv[:, 2 * HEAD_DIM:].astype(BF16)

        @pl.when(b >= 2)
        def _():
            for c in kv_store(b - 2):
                c.wait()

        for c in kv_store(b):
            c.start()

        for n in range(tokens // KEYS):
            @pl.when(b * ROWS // KEYS == n)
            def _(n=n):
                attend(q, b, (n + 1) * KEYS)

        @pl.when(b == 0)
        def _():
            for c in w_loads[3:]:
                c.wait()

        gate = jnp.dot(a, wg[...], preferred_element_type=F32)
        up = jnp.dot(a, wu[...], preferred_element_type=F32)
        ombuf[:, pl.ds(HEAD_DIM, ff)] = (gate * jax.nn.sigmoid(gate) * up).astype(BF16)

        @pl.when(b >= 2)
        def _():
            pair_copy(b - 2).wait_send()

        om = ombuf[...]
        for c0 in range(0, width, OUT_TILE):
            cols = pl.ds(c0, OUT_TILE)
            part[slot, :, cols] = jnp.dot(om, wod[:, cols], preferred_element_type=F32).astype(BF16)
        pair_copy(b).start()

    def add(dst, *srcs):
        total = dst[...].astype(F32)
        for s in srcs:
            total = total + s[...].astype(F32)
        dst[...] = total.astype(BF16)

    def both(f):
        for ab in (0, 1):
            for d in (0, 1):
                f(ab, d)

    def stage1(b):
        pair_copy(b).wait_recv()
        mine = pl.ds(pl.multiple_of(mine0, half), half)
        for r in range(0, ROWS, 32):
            add(quart.at[b, pl.ds(r, 32), :], part.at[lax.rem(b, 2), pl.ds(r, 32), mine])
        issue(send1, b)

    def stage2(b):
        both(lambda ab, d: send1(b, ab, d).wait_recv())
        both(lambda ab, d: add(quart.at[b, :, qcols(ab, pos[ab] + 1 - 2 * d, d)], r1.at[b, ab, d]))
        issue(send2, b)

    def stage3(b):
        both(lambda ab, d: send2(b, ab, d).wait_recv())
        for ab in (0, 1):
            add(quart.at[b, :, qcols(ab, pos[ab])], r2.at[b, ab, 0], r2.at[b, ab, 1])
        issue(send3, b)

    def stage4(b):
        both(lambda ab, d: send3(b, ab, d).wait_recv())
        both(lambda ab, d: add(quart.at[b, brows(pos[1 - ab] + 1 - 2 * d), qcols(ab, pos[ab], d)], r3.at[b, ab, d]))
        issue(send4, b)

    def stage5(b):
        @pl.when(b == 0)
        def _():
            for c in res_loads:
                c.wait()

        both(lambda ab, d: send4(b, ab, d).wait_recv())
        for ab in (0, 1):
            p2 = pos[1 - ab]
            total = quart[b, brows(p2), qcols(ab, pos[ab])].astype(F32)
            total = total + r4[b, ab, 0].astype(F32) + r4[b, ab, 1].astype(F32)
            total = total + xres[ab, yrows(b, p2), :].astype(F32)
            ybuf[yrows(b, p2), ycols(ab, pos[ab])] = total.astype(BF16)
        issue(send5, b)

    def stage6(b):
        both(lambda ab, d: land5(b, ab, d).wait_recv())
        issue(send6, b)

    def stage7(b):
        both(lambda ab, d: land6(b, ab, d).wait_recv())
        issue(send7, b)

    def stage8(b):
        both(lambda ab, d: land7(b, ab, d).wait_recv())
        issue(send8, b)

    def stage9(b):
        both(lambda ab, d: land8(b, ab, d).wait_recv())

        @pl.when(b >= 2)
        def _():
            gpair(b - 2, core).wait_send()

        gpair(b, core).start()

    def stage10(b):
        gpair(b, 1 - core).wait_recv()

        @pl.when(b >= 2)
        def _():
            y_store(b - 2).wait()

        y_store(b).start()

    stages = (compute, stage1, stage2, stage3, stage4, stage5, stage6, stage7, stage8, stage9, stage10)

    pl.semaphore_wait(barrier, 5)

    @pl.loop(0, nblk + LAG[-1])
    def _(t):
        for lag, stage in zip(LAG, stages):
            b = t - lag

            @pl.when((b >= 0) & (b < nblk))
            def _(b=b, stage=stage):
                stage(b)

    for b in range(nblk - 2, nblk):
        pair_copy(b).wait_send()
        for send in sends:
            both(lambda ab, d: send(b, ab, d).wait_send())
        gpair(b, core).wait_send()
        y_store(b).wait()
        for c in kv_store(b):
            c.wait()


def solution(mesh):
    tp_size = mesh.shape['tp']
    side = math.isqrt(tp_size // 2)

    def local_layer(x_in, g_norm, w_q, w_k, w_v, w_o, w_gate, w_up, w_down):
        tokens, width = x_in.shape
        kv_heads = w_k.shape[1] // HEAD_DIM
        ff = w_gate.shape[1]
        nblk = tokens // ROWS
        half = width // 2
        cw = half // 2 // side
        rw = ROWS // side
        inv_freq = ROPE_BASE ** (-jnp.arange(0, HEAD_DIM, 2, dtype=F32) / HEAD_DIM)
        angles = jnp.arange(tokens).astype(F32)[:, None] * inv_freq[None, :]
        cos_half, sin_half = jnp.cos(angles), jnp.sin(angles)
        cos_tab = jnp.concatenate([cos_half, cos_half], axis=1)
        sin_tab = jnp.concatenate([-sin_half, sin_half], axis=1)
        any_spec = pl.BlockSpec(memory_space=pl.ANY)
        y, k, v = pl.pallas_call(
            functools.partial(layer_kernel, (tp_size, side, kv_heads)),
            out_shape=(jax.ShapeDtypeStruct((tokens, width), BF16),
                       jax.ShapeDtypeStruct((tokens, HEAD_DIM), BF16),
                       jax.ShapeDtypeStruct((tokens, HEAD_DIM), BF16)),
            in_specs=[any_spec, pl.BlockSpec(memory_space=pltpu.VMEM)] + [any_spec] * 9,
            out_specs=(any_spec,) * 3,
            scratch_shapes=[
                pltpu.VMEM((width, 3 * HEAD_DIM), BF16),
                pltpu.VMEM((width, ff), BF16),
                pltpu.VMEM((width, ff), BF16),
                pltpu.VMEM((HEAD_DIM + ff, width), BF16),
                pltpu.VMEM((2, ROWS, width), BF16),
                pltpu.VMEM((2, 2, ROWS, HEAD_DIM), F32),
                pltpu.VMEM((ROWS, width), BF16),
                pltpu.VMEM((ROWS, HEAD_DIM + ff), BF16),
                pltpu.VMEM((tokens, HEAD_DIM), BF16),
                pltpu.VMEM((tokens, HEAD_DIM), BF16),
                pltpu.VMEM((2, ROWS, width), BF16),
                pltpu.VMEM((nblk, ROWS, half), BF16),
                pltpu.VMEM((nblk, 2, 2, ROWS, cw // 2), BF16),
                pltpu.VMEM((nblk, 2, 2, ROWS, cw), BF16),
                pltpu.VMEM((nblk, 2, 2, rw, cw // 2), BF16),
                pltpu.VMEM((nblk, 2, 2, rw, cw), BF16),
                pltpu.VMEM((2, tokens, cw), BF16),
                pltpu.VMEM((tokens, width), BF16),
                pltpu.SemaphoreType.DMA((7,)),
                pltpu.SemaphoreType.DMA((2, 3)),
                pltpu.SemaphoreType.DMA((2,)),
                pltpu.SemaphoreType.DMA((2, 2)),
                pltpu.SemaphoreType.DMA((2,)),
                pltpu.SemaphoreType.DMA((2,)),
                pltpu.SemaphoreType.DMA((nblk,)),
                pltpu.SemaphoreType.DMA((8, 2, 2, 2)),
                pltpu.SemaphoreType.DMA((8, 2, 2, nblk)),
                pltpu.SemaphoreType.DMA((2,)),
                pltpu.SemaphoreType.DMA((nblk,)),
            ],
            compiler_params=pltpu.CompilerParams(collective_id=0, has_side_effects=True, vmem_limit_bytes=67043328),
            name="layer",
        )(x_in, g_norm.reshape(1, width), cos_tab, sin_tab, w_q, w_k, w_v, w_o, w_gate, w_up, w_down)
        return y, k.reshape(tokens, 1, HEAD_DIM), v.reshape(tokens, 1, HEAD_DIM)

    return jax.shard_map(local_layer, mesh=mesh, in_specs=(P('dp', None), P(None), P(None, 'tp'), P(None, None), P(None, None), P('tp', None), P(None, 'tp'), P(None, 'tp'), P('tp', None)), out_specs=(P('dp', None), P('dp', 'tp', None), P('dp', 'tp', None)), check_vma=False)
```

time: 563 us -> 173 us (0.31)
  matrix products: 286 us -> 0 us
  waiting for transfers between devices: 171 us -> 0 us
  Pallas kernels: 0 us -> 136 us
  other arithmetic: 64.9 us -> 5.67 us
  local copies, waits for them, and re-layouts: 11.5 us -> 29.8 us
  between operations: 14.2 us -> 0.67 us
  loops' own time: 11.7 us -> 0 us
    dot_general x82 -> x0, matrix products: 286 us -> none  [the longest x16 116 us: row_block(): jnp.dot(hidden, w_down, preferred_element_type=jnp.float32)]
    psum x1 -> x0, waiting for transfers between devices: 170 us -> none  [local_layer(): reduced_sum = lax.psum(partial_sum, 'tp')]
    pallas_call x0 -> x1, Pallas kernels: none -> 136 us  [local_layer(): pl.pallas_call(functools.partial(layer_kernel, (tp_size, side, kv_heads))...]
    convert_element_type x4 -> x1, other arithmetic: 34.8 us -> 0.01 us  [local_layer(): angles = jnp.arange(tokens).astype(F32)[:, None] * inv_freq[None, :]]
    unnamed x3 -> x9, local copies, waits for them, and re-layouts: 1 us -> 28.5 us
    reduce_sum x17 -> x0, other arithmetic: 12.1 us -> none  [the longest x1 7.21 us: rms_norm(): jnp.mean(x_f32 * x_f32, axis=-1, keepdims=True) + NORM_EPS]
    another operation x1 -> x0, loops' own time: 11.7 us -> none  [local_layer(): lax.map(row_block, jnp.arange(tokens // q_block)).reshape(tokens, width)]
    concatenate x17 -> x1, other arithmetic: 12.8 us -> 1.93 us  [local_layer(): cos_tab = jnp.concatenate([cos_half, cos_half], axis=1)]
  transfers between devices with their start and end apart: 1 -> 0, of which waited for: 1 -> 0; matrix products, arithmetic and copies ran while one was open for 0% -> 0% of each run, Pallas kernels for 0% -> 0%
where the time goes in v1:
time: 173 us; the launch traced here: 172 us
  Pallas kernels  136 us (79%)
  local copies, waits for them, and re-layouts  29.8 us (17%)
  other arithmetic  5.67 us (3%)
    pallas_call x1, Pallas kernels, local_layer(): pl.pallas_call(functools.partial(layer_kernel, (tp_size, side, kv_heads))...  136 us
    unnamed x9, local copies, waits for them, and re-layouts  28.5 us
    neg x1, other arithmetic, local_layer(): sin_tab = jnp.concatenate([-sin_half, sin_half], axis=1)  3.72 us

profile of v1, /device:TPU:97, one launch (start us, length us, event | category | flops | bytes accessed | tf_op | source)
XLA Modules:
  0.0 172.4 jit_solution(18313953082909481057)
XLA Ops:
  0.7 1.3 reshape.26.g_ref
  2.0 3.7 %fusion = (f32[2048,64]{1,0:T(8,128)S(1)}, f32[2048,64]{1,0:T(8,128)S(1)}, f32[2048,64]{1,0:T(8,128)S(1)}) fusion(f32[64]{0:T(128)S(1)} %multiply_power_fusion, f32[2048]{0:T(1024)S(1)} %iota_convert_fusion), kind=kLoop, calls=%fused_computation.4 | loop fusion | flops 262144 | bytes 1581312 | tf_op jit(solution)/shard_map/neg | solution.py:385
  5.7 1.9 %pad_maximum_fusion = (f32[2048,128]{1,0:T(8,128)}, f32[2048,128]{1,0:T(8,128)}) fusion(f32[2048,64]{1,0:T(8,128)S(1)} %get-tuple-element.11, f32[2048,64]{1,0:T(8,128)S(1)} %get-tuple-element.10, f32[2048,64]{1,0:T(8,128)S(1)} %get-tuple-element.9), kind=kLoop, calls=%fused_computation.2 | loop fusion | flops 524288 | bytes 3670016 | tf_op jit(solution)/shard_map/concatenate | solution.py:384
  7.6 6.3 %copy.12.wg_hbm = bf16[4096,448]{1,0:T(8,128)(2,1)} copy(bf16[4096,448]{0,1:T(8,128)(2,1)} %param.15) | data formatting | bytes 7340032 | tf_op args[6]
  14.0 6.5 %copy.13.wu_hbm = bf16[4096,448]{1,0:T(8,128)(2,1)} copy(bf16[4096,448]{0,1:T(8,128)(2,1)} %param.16) | data formatting | bytes 7340032 | tf_op args[7]
  20.4 136.3 %layer.1 = (bf16[2048,4096]{1,0:T(8,128)(2,1)}, bf16[2048,128]{1,0:T(8,128)(2,1)}, bf16[2048,128]{1,0:T(8,128)(2,1)}) custom-call(bf16[2048,4096]{1,0:T(8,128)(2,1)} %x_hbm.1, bf16[1,4096]{1,0:T(2,128)(2,1)} %reshape.26.g_ref, f32[2048,128]{1,0:T(8,128)} %get-tuple-element.12.cos_hbm, f32[2048,128]{1,0:T(8,128)} %get-tuple-element.13.sin_hbm, ...), custom_call_target="tpu_custom_call" | custom-call | tf_op jit(solution)/shard_map/layer/pallas_call | solution.py:387
  156.7 0.0 copy-start.1
  156.7 0.0 copy-start
  156.7 14.1 %copy.17 = bf16[2048,4096]{1,0:T(8,128)(2,1)} copy(bf16[2048,4096]{1,0:T(8,128)(2,1)} %get-tuple-element.17) | data formatting | bytes 33554432
  170.9 0.0 copy-done.1
  170.9 0.8 copy.18
  171.7 0.0 copy-done
  171.7 0.8 copy.19
  (2 shorter events, 0.0 us)
Async XLA Ops:
  156.7 14.2 %copy-start.1 = (bf16[2048,128]{1,0:T(8,128)(2,1)S(1)}, bf16[2048,128]{1,0:T(8,128)(2,1)}, u32[]{:S(2)}) copy-start(bf16[2048,128]{1,0:T(8,128)(2,1)} %get-tuple-element.7) | copy-start | bytes 1572868
  156.7 15.0 %copy-start = (bf16[2048,128]{1,0:T(8,128)(2,1)S(1)}, bf16[2048,128]{1,0:T(8,128)(2,1)}, u32[]{:S(2)}) copy-start(bf16[2048,128]{1,0:T(8,128)(2,1)} %get-tuple-element.8) | copy-start | bytes 1572868

commit v2 on v1

--- a/solution.py
+++ b/solution.py
@@ -2,6 +2,7 @@
 import math
 import jax
 import jax.numpy as jnp
+import numpy as np
 from jax import lax
 from jax.experimental import pallas as pl
 from jax.experimental.pallas import tpu as pltpu
@@ -12,17 +13,19 @@
 NORM_EPS = 1e-5
 LANES = 128
 ROWS = 128
+PAIR = 2 * ROWS
+SLOTS = 4
 KEYS = 512
 OUT_TILE = 1024
-LAG = (0, 1, 2, 3, 4, 5, 6, 7, 8, 9, 10)
+LAG = (2, 3, 4, 5, 6, 7, 8, 9, 10, 11)
 BF16 = jnp.bfloat16
 F32 = jnp.float32
 
 
-def layer_kernel(cfg, x_hbm, g_ref, cos_hbm, sin_hbm, wq_hbm, wk_hbm, wv_hbm, wo_hbm, wg_hbm, wu_hbm, wd_hbm,
-                 y_hbm, k_hbm, v_hbm,
-                 wqkv, wg, wu, wod, xbuf, tabs, abuf, ombuf, kbuf, vbuf, part, quart, r1, r2, r3, r4, xres, ybuf,
-                 wsem, xsem, ressem, kvsem, ysem, pair_send, pair_recv, ssem, rsem, gpair_send, gpair_recv):
+def layer_kernel(cfg, x_hbm, g_ref, tab_hbm, wq_hbm, wk_hbm, wv_hbm, wo_hbm, wg_hbm, wu_hbm, wd_hbm,
+                 ybuf, k_hbm, v_hbm,
+                 wqkv, wgu, wod, xbuf, tabs, abuf, ombuf, kbuf, vbuf, part, quart, r1, r2, r3, r4, xres,
+                 wsem, xsem, ressem, kvsem, pair_send, pair_recv, ssem, rsem, gpair_send, gpair_recv):
     tokens, width = x_hbm.shape
     tp, side, kv_heads = cfg
     nblk = tokens // ROWS
@@ -31,7 +34,7 @@
     cw = quarter // side
     ch = cw // 2
     rw = ROWS // side
-    ff = wg.shape[1]
+    ff = wg_hbm.shape[0]
 
     me = lax.axis_index("tp")
     core = lax.rem(me, 2)
@@ -60,18 +63,17 @@
     mine0 = core * half
     res_col = [pl.multiple_of(mine0 + ab * quarter + pos[ab] * cw, cw) for ab in (0, 1)]
 
-    def x_load(b, slot):
-        rows = pl.ds(pl.multiple_of(b * ROWS, ROWS), ROWS)
+    def x_load(c, slot):
+        rows = pl.ds(pl.multiple_of(c * PAIR, PAIR), PAIR)
         return (pltpu.make_async_copy(x_hbm.at[rows], xbuf.at[slot], xsem.at[slot, 0]),
-                pltpu.make_async_copy(cos_hbm.at[rows], tabs.at[slot, 0], xsem.at[slot, 1]),
-                pltpu.make_async_copy(sin_hbm.at[rows], tabs.at[slot, 1], xsem.at[slot, 2]))
+                pltpu.make_async_copy(tab_hbm.at[:, rows], tabs.at[slot], xsem.at[slot, 1]))
 
     w_loads = (
         pltpu.make_async_copy(wq_hbm, wqkv.at[:, pl.ds(0, HEAD_DIM)], wsem.at[0]),
         pltpu.make_async_copy(wk_hbm.at[:, kcol], wqkv.at[:, pl.ds(HEAD_DIM, HEAD_DIM)], wsem.at[1]),
         pltpu.make_async_copy(wv_hbm.at[:, kcol], wqkv.at[:, pl.ds(2 * HEAD_DIM, HEAD_DIM)], wsem.at[2]),
-        pltpu.make_async_copy(wg_hbm, wg, wsem.at[3]),
-        pltpu.make_async_copy(wu_hbm, wu, wsem.at[4]),
+        pltpu.make_async_copy(wg_hbm, wgu.at[pl.ds(0, ff)], wsem.at[3]),
+        pltpu.make_async_copy(wu_hbm, wgu.at[pl.ds(ff, ff)], wsem.at[4]),
         pltpu.make_async_copy(wo_hbm, wod.at[pl.ds(0, HEAD_DIM)], wsem.at[5]),
         pltpu.make_async_copy(wd_hbm, wod.at[pl.ds(HEAD_DIM, ff)], wsem.at[6]),
     )
@@ -88,8 +90,8 @@
     def pair_copy(b):
         col = pl.multiple_of((1 - core) * half, half)
         return pltpu.make_async_remote_copy(
-            src_ref=part.at[lax.rem(b, 2), :, pl.ds(col, half)], dst_ref=quart.at[b],
-            send_sem=pair_send.at[lax.rem(b, 2)], recv_sem=pair_recv.at[b],
+            src_ref=part.at[lax.rem(b, SLOTS), :, pl.ds(col, half)], dst_ref=quart.at[b],
+            send_sem=pair_send.at[lax.rem(b, SLOTS)], recv_sem=pair_recv.at[b],
             device_id=dev(partner), device_id_type=pl.DeviceIdType.MESH)
 
     def hop(src, dst, st, b, ab, d, axis):
@@ -119,11 +121,11 @@
 
     def send1(b, ab, d):
         p = pos[ab]
-        return hop(quart.at[b, :, qcols(ab, p + 2, d)], r1.at[b, ab, d], 0, b, ab, d, ab)
+        return hop(quart.at[b, :, qcols(ab, p + 2, d)], r1.at[lax.rem(b, SLOTS), ab, d], 0, b, ab, d, ab)
 
     def send2(b, ab, d):
         p = pos[ab]
-        return hop(quart.at[b, :, qcols(ab, p + 1 - 2 * d)], r2.at[b, ab, d], 1, b, ab, d, ab)
+        return hop(quart.at[b, :, qcols(ab, p + 1 - 2 * d)], r2.at[lax.rem(b, SLOTS), ab, d], 1, b, ab, d, ab)
 
     def send3(b, ab, d):
         p2 = pos[1 - ab]
@@ -169,12 +171,9 @@
             send_sem=gpair_send.at[lax.rem(b, 2)], recv_sem=gpair_recv.at[b],
             device_id=dev(partner), device_id_type=pl.DeviceIdType.MESH)
 
-    def y_store(b):
-        return pltpu.make_async_copy(ybuf.at[yrows(b)], y_hbm.at[yrows(b)], ysem.at[lax.rem(b, 2)])
-
-    def kv_store(b):
-        rows = yrows(b)
-        slot = lax.rem(b, 2)
+    def kv_store(c):
+        rows = pl.ds(pl.multiple_of(c * PAIR, PAIR), PAIR)
+        slot = lax.rem(c, 2)
         return (pltpu.make_async_copy(kbuf.at[rows], k_hbm.at[rows], kvsem.at[slot, 0]),
                 pltpu.make_async_copy(vbuf.at[rows], v_hbm.at[rows], kvsem.at[slot, 1]))
 
@@ -186,11 +185,11 @@
                     send(b - 2, ab, d).wait_send()
                 send(b, ab, d).start()
 
-    def attend(q, b, keys):
+    def attend(q, c, keys):
         ks = kbuf[pl.ds(0, keys), :]
         s = lax.dot_general(q, ks, (((1,), (1,)), ((), ())), preferred_element_type=F32)
         s = s * (1.0 / math.sqrt(HEAD_DIM))
-        qpos = b * ROWS + lax.broadcasted_iota(jnp.int32, s.shape, 0)
+        qpos = c * PAIR + lax.broadcasted_iota(jnp.int32, s.shape, 0)
         kpos = lax.broadcasted_iota(jnp.int32, s.shape, 1)
         s = jnp.where(kpos <= qpos, s, -1e30)
         top = jnp.max(s, axis=-1, keepdims=True)
@@ -199,28 +198,29 @@
         o = jnp.dot(probs, vbuf[pl.ds(0, keys), :], preferred_element_type=F32)
         ombuf[:, pl.ds(0, HEAD_DIM)] = o.astype(BF16)
 
-    def compute(b):
-        slot = lax.rem(b, 2)
-        for c in x_load(b, slot):
-            c.wait()
-
-        @pl.when(b + 1 < nblk)
-        def _():
-            for c in x_load(b + 1, 1 - slot):
-                c.start()
-
-        @pl.when(b == 0)
-        def _():
-            for c in w_loads[:3]:
-                c.wait()
-
-        for r in range(0, ROWS, 16):
+    def compute_a(c):
+        slot = lax.rem(c, 2)
+        for cp in x_load(c, slot):
+            cp.wait()
+
+        @pl.when(c + 1 < nblk // 2)
+        def _():
+            for cp in x_load(c + 1, 1 - slot):
+                cp.start()
+
+        for r in range(0, PAIR, 16):
             xr = xbuf[slot, pl.ds(r, 16), :].astype(F32)
             inv = lax.rsqrt(jnp.mean(xr * xr, axis=-1, keepdims=True) + NORM_EPS)
-            abuf[pl.ds(r, 16), :] = (xr * inv * g_ref[...].astype(F32)).astype(BF16)
-
-        a = abuf[...]
-        qkv = jnp.dot(a, wqkv[...], preferred_element_type=F32)
+            for j in range(width // LANES):
+                cols = slice(j * LANES, (j + 1) * LANES)
+                abuf[pl.ds(r, 16), cols] = (xr[:, cols] * inv * g_ref[j:j + 1, :].astype(F32)).astype(BF16)
+
+        @pl.when(c == 0)
+        def _():
+            for cp in w_loads[:3]:
+                cp.wait()
+
+        qkv = jnp.dot(abuf[...], wqkv[...], preferred_element_type=F32)
         cos_t = tabs[slot, 0]
         sin_t = tabs[slot, 1]
 
@@ -228,41 +228,47 @@
             return (z * cos_t + pltpu.roll(z, HEAD_DIM // 2, 1) * sin_t).astype(BF16)
 
         q = rope(qkv[:, :HEAD_DIM])
-        rows = yrows(b)
+        rows = pl.ds(pl.multiple_of(c * PAIR, PAIR), PAIR)
         kbuf[rows, :] = rope(qkv[:, HEAD_DIM:2 * HEAD_DIM])
         vbuf[rows, :] = qkv[:, 2 * HEAD_DIM:].astype(BF16)
 
-        @pl.when(b >= 2)
-        def _():
-            for c in kv_store(b - 2):
-                c.wait()
-
-        for c in kv_store(b):
-            c.start()
+        @pl.when(c >= 2)
+        def _():
+            for cp in kv_store(c - 2):
+                cp.wait()
+
+        for cp in kv_store(c):
+            cp.start()
 
         for n in range(tokens // KEYS):
-            @pl.when(b * ROWS // KEYS == n)
+            @pl.when(c * PAIR // KEYS == n)
             def _(n=n):
-                attend(q, b, (n + 1) * KEYS)
-
-        @pl.when(b == 0)
-        def _():
-            for c in w_loads[3:]:
-                c.wait()
-
-        gate = jnp.dot(a, wg[...], preferred_element_type=F32)
-        up = jnp.dot(a, wu[...], preferred_element_type=F32)
-        ombuf[:, pl.ds(HEAD_DIM, ff)] = (gate * jax.nn.sigmoid(gate) * up).astype(BF16)
-
-        @pl.when(b >= 2)
-        def _():
-            pair_copy(b - 2).wait_send()
+                attend(q, c, (n + 1) * KEYS)
+
+    def compute_b(c):
+        @pl.when(c == 0)
+        def _():
+            for cp in w_loads[3:]:
+                cp.wait()
+
+        gu = lax.dot_general(wgu[...], abuf[...], (((1,), (1,)), ((), ())), preferred_element_type=F32)
+        gate, up = gu[:ff], gu[ff:]
+        hidden = gate * jax.nn.sigmoid(gate) * up
+        ombuf[:, pl.ds(HEAD_DIM, ff)] = hidden.T.astype(BF16)
+
+        @pl.when(c >= 2)
+        def _():
+            pair_copy(2 * c - 4).wait_send()
+            pair_copy(2 * c - 3).wait_send()
 
         om = ombuf[...]
         for c0 in range(0, width, OUT_TILE):
             cols = pl.ds(c0, OUT_TILE)
-            part[slot, :, cols] = jnp.dot(om, wod[:, cols], preferred_element_type=F32).astype(BF16)
-        pair_copy(b).start()
+            share = jnp.dot(om, wod[:, cols], preferred_element_type=F32).astype(BF16)
+            for i in (0, 1):
+                part[lax.rem(2 * c + i, SLOTS), :, cols] = share[i * ROWS:(i + 1) * ROWS]
+        pair_copy(2 * c).start()
+        pair_copy(2 * c + 1).start()
 
     def add(dst, *srcs):
         total = dst[...].astype(F32)
@@ -279,18 +285,18 @@
         pair_copy(b).wait_recv()
         mine = pl.ds(pl.multiple_of(mine0, half), half)
         for r in range(0, ROWS, 32):
-            add(quart.at[b, pl.ds(r, 32), :], part.at[lax.rem(b, 2), pl.ds(r, 32), mine])
+            add(quart.at[b, pl.ds(r, 32), :], part.at[lax.rem(b, SLOTS), pl.ds(r, 32), mine])
         issue(send1, b)
 
     def stage2(b):
         both(lambda ab, d: send1(b, ab, d).wait_recv())
-        both(lambda ab, d: add(quart.at[b, :, qcols(ab, pos[ab] + 1 - 2 * d, d)], r1.at[b, ab, d]))
+        both(lambda ab, d: add(quart.at[b, :, qcols(ab, pos[ab] + 1 - 2 * d, d)], r1.at[lax.rem(b, SLOTS), ab, d]))
         issue(send2, b)
 
     def stage3(b):
         both(lambda ab, d: send2(b, ab, d).wait_recv())
         for ab in (0, 1):
-            add(quart.at[b, :, qcols(ab, pos[ab])], r2.at[b, ab, 0], r2.at[b, ab, 1])
+            add(quart.at[b, :, qcols(ab, pos[ab])], r2.at[lax.rem(b, SLOTS), ab, 0], r2.at[lax.rem(b, SLOTS), ab, 1])
         issue(send3, b)
 
     def stage4(b):
@@ -337,18 +343,20 @@
     def stage10(b):
         gpair(b, 1 - core).wait_recv()
 
-        @pl.when(b >= 2)
-        def _():
-            y_store(b - 2).wait()
-
-        y_store(b).start()
-
-    stages = (compute, stage1, stage2, stage3, stage4, stage5, stage6, stage7, stage8, stage9, stage10)
+    stages = (stage1, stage2, stage3, stage4, stage5, stage6, stage7, stage8, stage9, stage10)
 
     pl.semaphore_wait(barrier, 5)
 
     @pl.loop(0, nblk + LAG[-1])
     def _(t):
+        @pl.when((t < nblk) & (lax.rem(t, 2) == 0))
+        def _():
+            compute_a(t // 2)
+
+        @pl.when((t < nblk) & (lax.rem(t, 2) == 1))
+        def _():
+            compute_b(t // 2)
+
         for lag, stage in zip(LAG, stages):
             b = t - lag
 
@@ -356,14 +364,22 @@
             def _(b=b, stage=stage):
                 stage(b)
 
+    for b in range(nblk - SLOTS, nblk):
+        pair_copy(b).wait_send()
     for b in range(nblk - 2, nblk):
-        pair_copy(b).wait_send()
         for send in sends:
             both(lambda ab, d: send(b, ab, d).wait_send())
         gpair(b, core).wait_send()
-        y_store(b).wait()
-        for c in kv_store(b):
-            c.wait()
+    for c in range(nblk // 2 - 2, nblk // 2):
+        for cp in kv_store(c):
+            cp.wait()
+
+
+def rope_tables(tokens):
+    inv_freq = np.float32(ROPE_BASE) ** (-np.arange(0, HEAD_DIM, 2, dtype=np.float32) / np.float32(HEAD_DIM))
+    angles = np.arange(tokens, dtype=np.float32)[:, None] * inv_freq[None, :]
+    cos_half, sin_half = np.cos(angles), np.sin(angles)
+    return np.stack([np.concatenate([cos_half, cos_half], axis=1), np.concatenate([-sin_half, sin_half], axis=1)])
 
 
 def solution(mesh):
@@ -378,53 +394,45 @@
         half = width // 2
         cw = half // 2 // side
         rw = ROWS // side
-        inv_freq = ROPE_BASE ** (-jnp.arange(0, HEAD_DIM, 2, dtype=F32) / HEAD_DIM)
-        angles = jnp.arange(tokens).astype(F32)[:, None] * inv_freq[None, :]
-        cos_half, sin_half = jnp.cos(angles), jnp.sin(angles)
-        cos_tab = jnp.concatenate([cos_half, cos_half], axis=1)
-        sin_tab = jnp.concatenate([-sin_half, sin_half], axis=1)
         any_spec = pl.BlockSpec(memory_space=pl.ANY)
         y, k, v = pl.pallas_call(
             functools.partial(layer_kernel, (tp_size, side, kv_heads)),
-            out_shape=(jax.ShapeDtypeStruct((tokens, width), BF16),
+            out_shape=(pltpu.VMEM((tokens, width), BF16),
                        jax.ShapeDtypeStruct((tokens, HEAD_DIM), BF16),
                        jax.ShapeDtypeStruct((tokens, HEAD_DIM), BF16)),
-            in_specs=[any_spec, pl.BlockSpec(memory_space=pltpu.VMEM)] + [any_spec] * 9,
-            out_specs=(any_spec,) * 3,
+            in_specs=[any_spec, pl.BlockSpec(memory_space=pltpu.VMEM)] + [any_spec] * 8,
+            out_specs=(pl.BlockSpec(memory_space=pltpu.VMEM), any_spec, any_spec),
             scratch_shapes=[
                 pltpu.VMEM((width, 3 * HEAD_DIM), BF16),
-                pltpu.VMEM((width, ff), BF16),
-                pltpu.VMEM((width, ff), BF16),
+                pltpu.VMEM((2 * ff, width), BF16),
                 pltpu.VMEM((HEAD_DIM + ff, width), BF16),
-                pltpu.VMEM((2, ROWS, width), BF16),
-                pltpu.VMEM((2, 2, ROWS, HEAD_DIM), F32),
-                pltpu.VMEM((ROWS, width), BF16),
-                pltpu.VMEM((ROWS, HEAD_DIM + ff), BF16),
+                pltpu.VMEM((2, PAIR, width), BF16),
+                pltpu.VMEM((2, 2, PAIR, HEAD_DIM), F32),
+                pltpu.VMEM((PAIR, width), BF16),
+                pltpu.VMEM((PAIR, HEAD_DIM + ff), BF16),
                 pltpu.VMEM((tokens, HEAD_DIM), BF16),
                 pltpu.VMEM((tokens, HEAD_DIM), BF16),
-                pltpu.VMEM((2, ROWS, width), BF16),
+                pltpu.VMEM((SLOTS, ROWS, width), BF16),
                 pltpu.VMEM((nblk, ROWS, half), BF16),
-                pltpu.VMEM((nblk, 2, 2, ROWS, cw // 2), BF16),
-                pltpu.VMEM((nblk, 2, 2, ROWS, cw), BF16),
+                pltpu.VMEM((SLOTS, 2, 2, ROWS, cw // 2), BF16),
+                pltpu.VMEM((SLOTS, 2, 2, ROWS, cw), BF16),
                 pltpu.VMEM((nblk, 2, 2, rw, cw // 2), BF16),
                 pltpu.VMEM((nblk, 2, 2, rw, cw), BF16),
                 pltpu.VMEM((2, tokens, cw), BF16),
-                pltpu.VMEM((tokens, width), BF16),
                 pltpu.SemaphoreType.DMA((7,)),
-                pltpu.SemaphoreType.DMA((2, 3)),
+                pltpu.SemaphoreType.DMA((2, 2)),
                 pltpu.SemaphoreType.DMA((2,)),
                 pltpu.SemaphoreType.DMA((2, 2)),
-                pltpu.SemaphoreType.DMA((2,)),
-                pltpu.SemaphoreType.DMA((2,)),
+                pltpu.SemaphoreType.DMA((SLOTS,)),
                 pltpu.SemaphoreType.DMA((nblk,)),
                 pltpu.SemaphoreType.DMA((8, 2, 2, 2)),
                 pltpu.SemaphoreType.DMA((8, 2, 2, nblk)),
                 pltpu.SemaphoreType.DMA((2,)),
                 pltpu.SemaphoreType.DMA((nblk,)),
             ],
-            compiler_params=pltpu.CompilerParams(collective_id=0, has_side_effects=True, vmem_limit_bytes=67043328),
+            compiler_params=pltpu.CompilerParams(collective_id=0, has_side_effects=True, vmem_limit_bytes=46 * 1024 * 1024),
             name="layer",
-        )(x_in, g_norm.reshape(1, width), cos_tab, sin_tab, w_q, w_k, w_v, w_o, w_gate, w_up, w_down)
+        )(x_in, g_norm.reshape(width // LANES, LANES), jnp.asarray(rope_tables(tokens)), w_q, w_k, w_v, w_o, w_gate.T, w_up.T, w_down)
         return y, k.reshape(tokens, 1, HEAD_DIM), v.reshape(tokens, 1, HEAD_DIM)
 
     return jax.shard_map(local_layer, mesh=mesh, in_specs=(P('dp', None), P(None), P(None, 'tp'), P(None, None), P(None, None), P('tp', None), P(None, 'tp'), P(None, 'tp'), P('tp', None)), out_specs=(P('dp', None), P('dp', 'tp', None), P('dp', 'tp', None)), check_vma=False)

time: 173 us -> 169 us (0.977)
  Pallas kernels: 136 us -> 160 us
  local copies, waits for them, and re-layouts: 29.8 us -> 7.76 us
  other arithmetic: 5.67 us -> 0 us
    pallas_call x1, Pallas kernels: 136 us -> 160 us  [local_layer(): pl.pallas_call(functools.partial(layer_kernel, (tp_size, side, kv_heads))...]
    unnamed x9 -> x7, local copies, waits for them, and re-layouts: 28.5 us -> 7.76 us
    neg x1 -> x0, other arithmetic: 3.72 us -> none  [local_layer(): sin_tab = jnp.concatenate([-sin_half, sin_half], axis=1)]
    concatenate x1 -> x0, other arithmetic: 1.93 us -> none  [local_layer(): cos_tab = jnp.concatenate([cos_half, cos_half], axis=1)]
where the time goes in v2:
time: 169 us
  Pallas kernels  160 us (95%)
  local copies, waits for them, and re-layouts  7.76 us (5%)
    pallas_call x1, Pallas kernels, local_layer(): pl.pallas_call(functools.partial(layer_kernel, (tp_size, side, kv_heads))...  160 us
    unnamed x7, local copies, waits for them, and re-layouts  7.76 us

profile of v2, /device:TPU:97, one launch (start us, length us, event | category | flops | bytes accessed | tf_op | source)
XLA Modules:
  0.0 168.8 jit_solution(2210802584540545593)
XLA Ops:
  0.6 160.4 %layer.1 = (bf16[2048,4096]{1,0:T(8,128)(2,1)S(1)}, bf16[2048,128]{1,0:T(8,128)(2,1)}, bf16[2048,128]{1,0:T(8,128)(2,1)}) custom-call(bf16[2048,4096]{1,0:T(8,128)(2,1)} %x_hbm.1, bf16[32,128]{1,0:T(8,128)(2,1)} %bitcast.9, f32[2,2048,128]{2,1,0:T(8,128)} %constant.2.clone.tab_hbm, bf16[4096,128]{1,0:T(8,128)(2,1)} %wq_hbm.1, bf16[4096,1024]{1,0:T(8,128)(2,1)} %wk_hbm.1, ...), custom_call_target="tpu_custom_call" | custom-call | tf_op jit(solution)/shard_map/layer/pallas_call | solution.py:398
  161.1 0.0 copy-start.1
  161.1 0.0 copy-start
  161.1 6.2 %copy.16 = bf16[2048,4096]{1,0:T(8,128)(2,1)} copy(bf16[2048,4096]{1,0:T(8,128)(2,1)S(1)} %get-tuple-element.9) | data formatting | bytes 33554432
  167.2 0.0 copy-done.1
  167.2 0.8 copy.17
  168.0 0.0 copy-done
  168.0 0.8 copy.18
Async XLA Ops:
  161.1 6.2 %copy-start.1 = (bf16[2048,128]{1,0:T(8,128)(2,1)S(1)}, bf16[2048,128]{1,0:T(8,128)(2,1)}, u32[]{:S(2)}) copy-start(bf16[2048,128]{1,0:T(8,128)(2,1)} %get-tuple-element.7) | copy-start | bytes 1572868
  161.1 7.0 %copy-start = (bf16[2048,128]{1,0:T(8,128)(2,1)S(1)}, bf16[2048,128]{1,0:T(8,128)(2,1)}, u32[]{:S(2)}) copy-start(bf16[2048,128]{1,0:T(8,128)(2,1)} %get-tuple-element.8) | copy-start | bytes 1572868

commit v3 on v2

--- a/solution.py
+++ b/solution.py
@@ -15,20 +15,24 @@
 ROWS = 128
 PAIR = 2 * ROWS
 SLOTS = 4
+RING = 4
 KEYS = 512
-OUT_TILE = 1024
+OUT_TILE = 512
 LAG = (2, 3, 4, 5, 6, 7, 8, 9, 10, 11)
+FIRST = (6, 7, 8, 9, 10)
+SECOND = (1, 2, 3, 4, 5)
 BF16 = jnp.bfloat16
 F32 = jnp.float32
 
 
 def layer_kernel(cfg, x_hbm, g_ref, tab_hbm, wq_hbm, wk_hbm, wv_hbm, wo_hbm, wg_hbm, wu_hbm, wd_hbm,
                  ybuf, k_hbm, v_hbm,
-                 wqkv, wgu, wod, xbuf, tabs, abuf, ombuf, kbuf, vbuf, part, quart, r1, r2, r3, r4, xres,
+                 wqkv, wall, wod, xbuf, tabs, abuf, atbuf, gbuf, qtbuf, ombuf, kbuf, vbuf, vtbuf, part, quart, r1, r2, r3, r4, xres,
                  wsem, xsem, ressem, kvsem, pair_send, pair_recv, ssem, rsem, gpair_send, gpair_recv):
     tokens, width = x_hbm.shape
-    tp, side, kv_heads = cfg
+    tp, side, kv_heads = cfg[:3]
     nblk = tokens // ROWS
+    npair = tokens // PAIR
     half = width // 2
     quarter = half // 2
     cw = quarter // side
@@ -65,15 +69,15 @@
 
     def x_load(c, slot):
         rows = pl.ds(pl.multiple_of(c * PAIR, PAIR), PAIR)
-        return (pltpu.make_async_copy(x_hbm.at[rows], xbuf.at[slot], xsem.at[slot, 0]),
-                pltpu.make_async_copy(tab_hbm.at[:, rows], tabs.at[slot], xsem.at[slot, 1]))
+        return (pltpu.make_async_copy(x_hbm.at[rows], xbuf, xsem.at[slot, 0]),
+                pltpu.make_async_copy(tab_hbm.at[:, :, rows], tabs.at[slot], xsem.at[slot, 1]))
 
     w_loads = (
-        pltpu.make_async_copy(wq_hbm, wqkv.at[:, pl.ds(0, HEAD_DIM)], wsem.at[0]),
-        pltpu.make_async_copy(wk_hbm.at[:, kcol], wqkv.at[:, pl.ds(HEAD_DIM, HEAD_DIM)], wsem.at[1]),
-        pltpu.make_async_copy(wv_hbm.at[:, kcol], wqkv.at[:, pl.ds(2 * HEAD_DIM, HEAD_DIM)], wsem.at[2]),
-        pltpu.make_async_copy(wg_hbm, wgu.at[pl.ds(0, ff)], wsem.at[3]),
-        pltpu.make_async_copy(wu_hbm, wgu.at[pl.ds(ff, ff)], wsem.at[4]),
+        pltpu.make_async_copy(wq_hbm, wqkv.at[0], wsem.at[0]),
+        pltpu.make_async_copy(wk_hbm.at[:, kcol], wqkv.at[1], wsem.at[1]),
+        pltpu.make_async_copy(wv_hbm.at[:, kcol], wqkv.at[2], wsem.at[2]),
+        pltpu.make_async_copy(wg_hbm, wall.at[pl.ds(3 * HEAD_DIM, ff)], wsem.at[3]),
+        pltpu.make_async_copy(wu_hbm, wall.at[pl.ds(3 * HEAD_DIM + ff, ff)], wsem.at[4]),
         pltpu.make_async_copy(wo_hbm, wod.at[pl.ds(0, HEAD_DIM)], wsem.at[5]),
         pltpu.make_async_copy(wd_hbm, wod.at[pl.ds(HEAD_DIM, ff)], wsem.at[6]),
     )
@@ -85,7 +89,7 @@
     for c in res_loads:
         c.start()
     kbuf[...] = jnp.zeros_like(kbuf)
-    vbuf[...] = jnp.zeros_like(vbuf)
+    vtbuf[...] = jnp.zeros_like(vtbuf)
 
     def pair_copy(b):
         col = pl.multiple_of((1 - core) * half, half)
@@ -121,11 +125,11 @@
 
     def send1(b, ab, d):
         p = pos[ab]
-        return hop(quart.at[b, :, qcols(ab, p + 2, d)], r1.at[lax.rem(b, SLOTS), ab, d], 0, b, ab, d, ab)
+        return hop(quart.at[b, :, qcols(ab, p + 2, d)], r1.at[lax.rem(b, RING), ab, d], 0, b, ab, d, ab)
 
     def send2(b, ab, d):
         p = pos[ab]
-        return hop(quart.at[b, :, qcols(ab, p + 1 - 2 * d)], r2.at[lax.rem(b, SLOTS), ab, d], 1, b, ab, d, ab)
+        return hop(quart.at[b, :, qcols(ab, p + 1 - 2 * d)], r2.at[lax.rem(b, RING), ab, d], 1, b, ab, d, ab)
 
     def send3(b, ab, d):
         p2 = pos[1 - ab]
@@ -175,98 +179,145 @@
         rows = pl.ds(pl.multiple_of(c * PAIR, PAIR), PAIR)
         slot = lax.rem(c, 2)
         return (pltpu.make_async_copy(kbuf.at[rows], k_hbm.at[rows], kvsem.at[slot, 0]),
-                pltpu.make_async_copy(vbuf.at[rows], v_hbm.at[rows], kvsem.at[slot, 1]))
+                pltpu.make_async_copy(vbuf.at[slot], v_hbm.at[rows], kvsem.at[slot, 1]))
 
     def issue(send, b):
-        for ab in (0, 1):
-            for d in (0, 1):
-                @pl.when(b >= 2)
-                def _():
-                    send(b - 2, ab, d).wait_send()
-                send(b, ab, d).start()
-
-    def attend(q, c, keys):
-        ks = kbuf[pl.ds(0, keys), :]
-        s = lax.dot_general(q, ks, (((1,), (1,)), ((), ())), preferred_element_type=F32)
-        s = s * (1.0 / math.sqrt(HEAD_DIM))
-        qpos = c * PAIR + lax.broadcasted_iota(jnp.int32, s.shape, 0)
-        kpos = lax.broadcasted_iota(jnp.int32, s.shape, 1)
-        s = jnp.where(kpos <= qpos, s, -1e30)
-        top = jnp.max(s, axis=-1, keepdims=True)
-        e = jnp.exp(s - top)
-        probs = (e * (1.0 / jnp.sum(e, axis=-1, keepdims=True))).astype(BF16)
-        o = jnp.dot(probs, vbuf[pl.ds(0, keys), :], preferred_element_type=F32)
-        ombuf[:, pl.ds(0, HEAD_DIM)] = o.astype(BF16)
-
-    def compute_a(c):
+        @pl.when(b >= 2)
+        def _():
+            both(lambda ab, d: send(b - 2, ab, d).wait_send())
+
+        both(lambda ab, d: send(b, ab, d).start())
+
+    def attend(q_t, c, keys):
+        s = jnp.dot(kbuf[pl.ds(0, keys), :], q_t, preferred_element_type=F32)
+        edge = keys - KEYS
+        tail = s[edge:]
+        kpos = edge + lax.broadcasted_iota(jnp.int32, tail.shape, 0)
+        qpos = c * PAIR + lax.broadcasted_iota(jnp.int32, tail.shape, 1)
+        tail = jnp.where(kpos <= qpos, tail, -1e30)
+        s = jnp.concatenate([s[:edge], tail], axis=0) if edge else tail
+        top = jnp.max(s, axis=0, keepdims=True)
+        e = jnp.exp2((s - top) * (math.log2(math.e) / math.sqrt(HEAD_DIM)))
+        probs = (e * (1.0 / jnp.sum(e, axis=0, keepdims=True))).astype(BF16)
+        o_t = jnp.dot(vtbuf[:, pl.ds(0, keys)], probs, preferred_element_type=F32)
+        ombuf[:, pl.ds(0, HEAD_DIM)] = o_t.T.astype(BF16)
+
+    def norm_rows(r):
+        xr = xbuf[pl.ds(r, 16), :].astype(F32)
+        inv = lax.rsqrt(jnp.mean(xr * xr, axis=-1, keepdims=True) + NORM_EPS)
+        for j in range(width // LANES):
+            cols = slice(j * LANES, (j + 1) * LANES)
+            abuf[pl.ds(r, 16), cols] = (xr[:, cols] * inv * gbuf[:, cols]).astype(BF16)
+
+    def turn(j):
+        cols = pl.ds(j * LANES, LANES)
+        atbuf[cols, :] = abuf[:, cols].T
+
+    def first_norm():
+        for j in range(width // LANES):
+            gbuf[:, j * LANES:(j + 1) * LANES] = jnp.broadcast_to(g_ref[j:j + 1, :].astype(F32), (16, LANES))
+
+        for cp in x_load(0, 0):
+            cp.wait()
+        @pl.loop(0, PAIR // 16)
+        def _(i):
+            norm_rows(pl.multiple_of(i * 16, 16))
+
+        for cp in x_load(1, 1):
+            cp.start()
+        for j in range(width // LANES):
+            turn(j)
+        for cp in w_loads[:3]:
+            cp.wait()
+        for r in range(0, width, 512):
+            for n in range(3):
+                wall[pl.ds(n * HEAD_DIM, HEAD_DIM), pl.ds(r, 512)] = wqkv[n, pl.ds(r, 512), :].T
+
+    def project(c):
         slot = lax.rem(c, 2)
-        for cp in x_load(c, slot):
-            cp.wait()
-
-        @pl.when(c + 1 < nblk // 2)
+
+        @pl.when(c + 1 < npair)
         def _():
             for cp in x_load(c + 1, 1 - slot):
-                cp.start()
-
-        for r in range(0, PAIR, 16):
-            xr = xbuf[slot, pl.ds(r, 16), :].astype(F32)
-            inv = lax.rsqrt(jnp.mean(xr * xr, axis=-1, keepdims=True) + NORM_EPS)
-            for j in range(width // LANES):
-                cols = slice(j * LANES, (j + 1) * LANES)
-                abuf[pl.ds(r, 16), cols] = (xr[:, cols] * inv * g_ref[j:j + 1, :].astype(F32)).astype(BF16)
-
-        @pl.when(c == 0)
-        def _():
-            for cp in w_loads[:3]:
                 cp.wait()
 
-        qkv = jnp.dot(abuf[...], wqkv[...], preferred_element_type=F32)
+        for r in range(0, PAIR // 2, 16):
+            norm_rows(r)
+        qkv = jnp.dot(wall[pl.ds(0, 3 * HEAD_DIM), :], atbuf[...], preferred_element_type=F32)
         cos_t = tabs[slot, 0]
         sin_t = tabs[slot, 1]
 
         def rope(z):
-            return (z * cos_t + pltpu.roll(z, HEAD_DIM // 2, 1) * sin_t).astype(BF16)
-
-        q = rope(qkv[:, :HEAD_DIM])
+            lo, hi = z[:HEAD_DIM // 2], z[HEAD_DIM // 2:]
+            return jnp.concatenate([lo * cos_t - hi * sin_t, hi * cos_t + lo * sin_t], axis=0)
+
+        qtbuf[...] = rope(qkv[:HEAD_DIM]).astype(BF16)
         rows = pl.ds(pl.multiple_of(c * PAIR, PAIR), PAIR)
-        kbuf[rows, :] = rope(qkv[:, HEAD_DIM:2 * HEAD_DIM])
-        vbuf[rows, :] = qkv[:, 2 * HEAD_DIM:].astype(BF16)
-
+        kbuf[rows, :] = rope(qkv[HEAD_DIM:2 * HEAD_DIM]).T.astype(BF16)
+        v_t = qkv[2 * HEAD_DIM:]
+        vtbuf[:, rows] = v_t.astype(BF16)
         @pl.when(c >= 2)
         def _():
             for cp in kv_store(c - 2):
                 cp.wait()
 
+        vbuf[slot] = v_t.T.astype(BF16)
         for cp in kv_store(c):
             cp.start()
+
+    def mix(c):
+        @pl.when(c == 0)
+        def _():
+            for cp in w_loads[3:5]:
+                cp.wait()
 
         for n in range(tokens // KEYS):
             @pl.when(c * PAIR // KEYS == n)
             def _(n=n):
-                attend(q, c, (n + 1) * KEYS)
-
-    def compute_b(c):
-        @pl.when(c == 0)
-        def _():
-            for cp in w_loads[3:]:
-                cp.wait()
-
-        gu = lax.dot_general(wgu[...], abuf[...], (((1,), (1,)), ((), ())), preferred_element_type=F32)
-        gate, up = gu[:ff], gu[ff:]
-        hidden = gate * jax.nn.sigmoid(gate) * up
-        ombuf[:, pl.ds(HEAD_DIM, ff)] = hidden.T.astype(BF16)
-
-        @pl.when(c >= 2)
-        def _():
-            pair_copy(2 * c - 4).wait_send()
-            pair_copy(2 * c - 3).wait_send()
-
+                attend(qtbuf[...], c, (n + 1) * KEYS)
+                gu = jnp.dot(wall[pl.ds(3 * HEAD_DIM, 2 * ff), :], atbuf[...], preferred_element_type=F32)
+                gate, up = gu[:ff], gu[ff:]
+                hidden = gate * jax.nn.sigmoid(gate) * up
+                ombuf[:, pl.ds(HEAD_DIM, ff)] = hidden.T.astype(BF16)
+
+    tiles = width // OUT_TILE
+
+    def out_tiles(c, first, last):
         om = ombuf[...]
-        for c0 in range(0, width, OUT_TILE):
-            cols = pl.ds(c0, OUT_TILE)
+        for n in range(first, last):
+            cols = pl.ds(n * OUT_TILE, OUT_TILE)
             share = jnp.dot(om, wod[:, cols], preferred_element_type=F32).astype(BF16)
             for i in (0, 1):
                 part[lax.rem(2 * c + i, SLOTS), :, cols] = share[i * ROWS:(i + 1) * ROWS]
+            early = tiles // 2
+            if n < early:
+                for r in range((early + n) * PAIR // tiles, (early + n + 1) * PAIR // tiles, 16):
+                    norm_rows(r)
+            else:
+                late = width // LANES // (tiles - early)
+                for j in range((n - early) * late, (n - early + 1) * late):
+                    turn(j)
+
+    def out_a(c):
+        @pl.when(c == 0)
+        def _():
+            for cp in w_loads[5:]:
+                cp.wait()
+
+        @pl.when(c >= 2)
+        def _():
+            pair_copy(2 * c - 4).wait_send()
+            pair_copy(2 * c - 3).wait_send()
+
+        out_tiles(c, 0, tiles // 2)
+
+        @pl.when(c + 2 < npair)
+        def _():
+            for cp in x_load(c + 2, lax.rem(c, 2)):
+                cp.start()
+
+    def out_b(c):
+        out_tiles(c, tiles // 2, tiles)
         pair_copy(2 * c).start()
         pair_copy(2 * c + 1).start()
 
@@ -290,13 +341,13 @@
 
     def stage2(b):
         both(lambda ab, d: send1(b, ab, d).wait_recv())
-        both(lambda ab, d: add(quart.at[b, :, qcols(ab, pos[ab] + 1 - 2 * d, d)], r1.at[lax.rem(b, SLOTS), ab, d]))
+        both(lambda ab, d: add(quart.at[b, :, qcols(ab, pos[ab] + 1 - 2 * d, d)], r1.at[lax.rem(b, RING), ab, d]))
         issue(send2, b)
 
     def stage3(b):
         both(lambda ab, d: send2(b, ab, d).wait_recv())
         for ab in (0, 1):
-            add(quart.at[b, :, qcols(ab, pos[ab])], r2.at[lax.rem(b, SLOTS), ab, 0], r2.at[lax.rem(b, SLOTS), ab, 1])
+            add(quart.at[b, :, qcols(ab, pos[ab])], r2.at[lax.rem(b, RING), ab, 0], r2.at[lax.rem(b, RING), ab, 1])
         issue(send3, b)
 
     def stage4(b):
@@ -345,24 +396,30 @@
 
     stages = (stage1, stage2, stage3, stage4, stage5, stage6, stage7, stage8, stage9, stage10)
 
+    first_norm()
     pl.semaphore_wait(barrier, 5)
 
     @pl.loop(0, nblk + LAG[-1])
     def _(t):
-        @pl.when((t < nblk) & (lax.rem(t, 2) == 0))
-        def _():
-            compute_a(t // 2)
-
-        @pl.when((t < nblk) & (lax.rem(t, 2) == 1))
-        def _():
-            compute_b(t // 2)
-
-        for lag, stage in zip(LAG, stages):
-            b = t - lag
-
-            @pl.when((b >= 0) & (b < nblk))
-            def _(b=b, stage=stage):
-                stage(b)
+        def run(group):
+            for n in group:
+                b = t - LAG[n - 1]
+
+                @pl.when((b >= 0) & (b < nblk))
+                def _(b=b, n=n):
+                    stages[n - 1](b)
+
+        def work(parity, piece):
+            @pl.when((t < nblk) & (lax.rem(t, 2) == parity))
+            def _():
+                piece(t // 2)
+
+        work(0, project)
+        work(1, out_a)
+        run(FIRST)
+        work(0, mix)
+        work(1, out_b)
+        run(SECOND)
 
     for b in range(nblk - SLOTS, nblk):
         pair_copy(b).wait_send()
@@ -378,8 +435,7 @@
 def rope_tables(tokens):
     inv_freq = np.float32(ROPE_BASE) ** (-np.arange(0, HEAD_DIM, 2, dtype=np.float32) / np.float32(HEAD_DIM))
     angles = np.arange(tokens, dtype=np.float32)[:, None] * inv_freq[None, :]
-    cos_half, sin_half = np.cos(angles), np.sin(angles)
-    return np.stack([np.concatenate([cos_half, cos_half], axis=1), np.concatenate([-sin_half, sin_half], axis=1)])
+    return np.stack([np.cos(angles).T, np.sin(angles).T])
 
 
 def solution(mesh):
@@ -403,19 +459,23 @@
             in_specs=[any_spec, pl.BlockSpec(memory_space=pltpu.VMEM)] + [any_spec] * 8,
             out_specs=(pl.BlockSpec(memory_space=pltpu.VMEM), any_spec, any_spec),
             scratch_shapes=[
-                pltpu.VMEM((width, 3 * HEAD_DIM), BF16),
-                pltpu.VMEM((2 * ff, width), BF16),
+                pltpu.VMEM((3, width, HEAD_DIM), BF16),
+                pltpu.VMEM((3 * HEAD_DIM + 2 * ff, width), BF16),
                 pltpu.VMEM((HEAD_DIM + ff, width), BF16),
-                pltpu.VMEM((2, PAIR, width), BF16),
-                pltpu.VMEM((2, 2, PAIR, HEAD_DIM), F32),
                 pltpu.VMEM((PAIR, width), BF16),
+                pltpu.VMEM((2, 2, HEAD_DIM // 2, PAIR), F32),
+                pltpu.VMEM((PAIR, width), BF16),
+                pltpu.VMEM((width, PAIR), BF16),
+                pltpu.VMEM((16, width), F32),
+                pltpu.VMEM((HEAD_DIM, PAIR), BF16),
                 pltpu.VMEM((PAIR, HEAD_DIM + ff), BF16),
                 pltpu.VMEM((tokens, HEAD_DIM), BF16),
-                pltpu.VMEM((tokens, HEAD_DIM), BF16),
+                pltpu.VMEM((2, PAIR, HEAD_DIM), BF16),
+                pltpu.VMEM((HEAD_DIM, tokens), BF16),
                 pltpu.VMEM((SLOTS, ROWS, width), BF16),
                 pltpu.VMEM((nblk, ROWS, half), BF16),
-                pltpu.VMEM((SLOTS, 2, 2, ROWS, cw // 2), BF16),
-                pltpu.VMEM((SLOTS, 2, 2, ROWS, cw), BF16),
+                pltpu.VMEM((RING, 2, 2, ROWS, cw // 2), BF16),
+                pltpu.VMEM((RING, 2, 2, ROWS, cw), BF16),
                 pltpu.VMEM((nblk, 2, 2, rw, cw // 2), BF16),
                 pltpu.VMEM((nblk, 2, 2, rw, cw), BF16),
                 pltpu.VMEM((2, tokens, cw), BF16),
@@ -430,7 +490,7 @@
                 pltpu.SemaphoreType.DMA((2,)),
                 pltpu.SemaphoreType.DMA((nblk,)),
             ],
-            compiler_params=pltpu.CompilerParams(collective_id=0, has_side_effects=True, vmem_limit_bytes=46 * 1024 * 1024),
+            compiler_params=pltpu.CompilerParams(collective_id=0, has_side_effects=True, vmem_limit_bytes=47 * 1024 * 1024),
             name="layer",
         )(x_in, g_norm.reshape(width // LANES, LANES), jnp.asarray(rope_tables(tokens)), w_q, w_k, w_v, w_o, w_gate.T, w_up.T, w_down)
         return y, k.reshape(tokens, 1, HEAD_DIM), v.reshape(tokens, 1, HEAD_DIM)

time: 169 us -> 185 us (1.095)
  Pallas kernels: 160 us -> 176 us
    pallas_call x1, Pallas kernels: 160 us -> 176 us  [local_layer(): pl.pallas_call(functools.partial(layer_kernel, (tp_size, side, kv_heads))...]
where the time goes in v3:
time: 185 us
  Pallas kernels  176 us (95%)
  local copies, waits for them, and re-layouts  7.76 us (4%)
    pallas_call x1, Pallas kernels, local_layer(): pl.pallas_call(functools.partial(layer_kernel, (tp_size, side, kv_heads))...  176 us
    unnamed x7, local copies, waits for them, and re-layouts  7.76 us

profile of v3, /device:TPU:97, one launch (start us, length us, event | category | flops | bytes accessed | tf_op | source)
XLA Modules:
  0.0 184.8 jit_solution(7328049741545730725)
XLA Ops:
  0.6 176.4 %layer.1 = (bf16[2048,4096]{1,0:T(8,128)(2,1)S(1)}, bf16[2048,128]{1,0:T(8,128)(2,1)}, bf16[2048,128]{1,0:T(8,128)(2,1)}) custom-call(bf16[2048,4096]{1,0:T(8,128)(2,1)} %x_hbm.1, bf16[32,128]{1,0:T(8,128)(2,1)} %bitcast.9, f32[2,64,2048]{2,1,0:T(8,128)} %constant.2.clone.tab_hbm, bf16[4096,128]{1,0:T(8,128)(2,1)} %wq_hbm.1, bf16[4096,1024]{1,0:T(8,128)(2,1)} %wk_hbm.1, ...), custom_call_target="tpu_custom_call" | custom-call | tf_op jit(solution)/shard_map/layer/pallas_call | solution.py:454
  177.1 0.0 copy-start.1
  177.1 0.0 copy-start
  177.1 6.2 %copy.16 = bf16[2048,4096]{1,0:T(8,128)(2,1)} copy(bf16[2048,4096]{1,0:T(8,128)(2,1)S(1)} %get-tuple-element.9) | data formatting | bytes 33554432
  183.2 0.0 copy-done.1
  183.2 0.8 copy.17
  184.0 0.0 copy-done
  184.0 0.8 copy.18
Async XLA Ops:
  177.1 6.2 %copy-start.1 = (bf16[2048,128]{1,0:T(8,128)(2,1)S(1)}, bf16[2048,128]{1,0:T(8,128)(2,1)}, u32[]{:S(2)}) copy-start(bf16[2048,128]{1,0:T(8,128)(2,1)} %get-tuple-element.7) | copy-start | bytes 1572868
  177.1 7.0 %copy-start = (bf16[2048,128]{1,0:T(8,128)(2,1)S(1)}, bf16[2048,128]{1,0:T(8,128)(2,1)}, u32[]{:S(2)}) copy-start(bf16[2048,128]{1,0:T(8,128)(2,1)} %get-tuple-element.8) | copy-start | bytes 1572868

commit v4 on v3

--- a/solution.py
+++ b/solution.py
@@ -14,20 +14,18 @@
 LANES = 128
 ROWS = 128
 PAIR = 2 * ROWS
-SLOTS = 4
+SLOTS = 2
 RING = 4
 KEYS = 512
 OUT_TILE = 512
 LAG = (2, 3, 4, 5, 6, 7, 8, 9, 10, 11)
-FIRST = (6, 7, 8, 9, 10)
-SECOND = (1, 2, 3, 4, 5)
 BF16 = jnp.bfloat16
 F32 = jnp.float32
 
 
 def layer_kernel(cfg, x_hbm, g_ref, tab_hbm, wq_hbm, wk_hbm, wv_hbm, wo_hbm, wg_hbm, wu_hbm, wd_hbm,
                  ybuf, k_hbm, v_hbm,
-                 wqkv, wall, wod, xbuf, tabs, abuf, atbuf, gbuf, qtbuf, ombuf, kbuf, vbuf, vtbuf, part, quart, r1, r2, r3, r4, xres,
+                 wqkv, wall, wod, xbuf, tabs, abuf, atbuf, gbuf, qtbuf, silu, ombuf, kbuf, vbuf, vtbuf, part, quart, r1, r2, r3, r4, xres,
                  wsem, xsem, ressem, kvsem, pair_send, pair_recv, ssem, rsem, gpair_send, gpair_recv):
     tokens, width = x_hbm.shape
     tp, side, kv_heads = cfg[:3]
@@ -175,6 +173,10 @@
             send_sem=gpair_send.at[lax.rem(b, 2)], recv_sem=gpair_recv.at[b],
             device_id=dev(partner), device_id_type=pl.DeviceIdType.MESH)
 
+    def wait_all(copies):
+        for cp in copies:
+            cp.wait()
+
     def kv_store(c):
         rows = pl.ds(pl.multiple_of(c * PAIR, PAIR), PAIR)
         slot = lax.rem(c, 2)
@@ -203,11 +205,16 @@
         ombuf[:, pl.ds(0, HEAD_DIM)] = o_t.T.astype(BF16)
 
     def norm_rows(r):
-        xr = xbuf[pl.ds(r, 16), :].astype(F32)
-        inv = lax.rsqrt(jnp.mean(xr * xr, axis=-1, keepdims=True) + NORM_EPS)
+        rows = pl.ds(r, 16)
+        sums = [jnp.zeros((16, LANES), F32)] * 2
         for j in range(width // LANES):
-            cols = slice(j * LANES, (j + 1) * LANES)
-            abuf[pl.ds(r, 16), cols] = (xr[:, cols] * inv * gbuf[:, cols]).astype(BF16)
+            xr = xbuf[rows, pl.ds(j * LANES, LANES)].astype(F32)
+            sums[j % 2] = sums[j % 2] + xr * xr
+        mean = jnp.sum(sums[0] + sums[1], axis=-1, keepdims=True) * (1.0 / width)
+        inv = jnp.broadcast_to(lax.rsqrt(mean + NORM_EPS), (16, LANES))
+        for j in range(width // LANES):
+            cols = pl.ds(j * LANES, LANES)
+            abuf[rows, cols] = (xbuf[rows, cols].astype(F32) * inv * gbuf[:, cols]).astype(BF16)
 
     def turn(j):
         cols = pl.ds(j * LANES, LANES)
@@ -235,14 +242,6 @@
 
     def project(c):
         slot = lax.rem(c, 2)
-
-        @pl.when(c + 1 < npair)
-        def _():
-            for cp in x_load(c + 1, 1 - slot):
-                cp.wait()
-
-        for r in range(0, PAIR // 2, 16):
-            norm_rows(r)
         qkv = jnp.dot(wall[pl.ds(0, 3 * HEAD_DIM), :], atbuf[...], preferred_element_type=F32)
         cos_t = tabs[slot, 0]
         sin_t = tabs[slot, 1]
@@ -265,61 +264,44 @@
         for cp in kv_store(c):
             cp.start()
 
+    def open_gate(c):
+        @pl.when(c == 0)
+        def _():
+            wait_all(w_loads[3:4])
+
+        gate = jnp.dot(wall[pl.ds(3 * HEAD_DIM, ff), :], atbuf[...], preferred_element_type=F32)
+        silu[...] = gate * jax.nn.sigmoid(gate)
+
     def mix(c):
         @pl.when(c == 0)
         def _():
-            for cp in w_loads[3:5]:
-                cp.wait()
+            wait_all(w_loads[4:])
 
         for n in range(tokens // KEYS):
             @pl.when(c * PAIR // KEYS == n)
             def _(n=n):
                 attend(qtbuf[...], c, (n + 1) * KEYS)
-                gu = jnp.dot(wall[pl.ds(3 * HEAD_DIM, 2 * ff), :], atbuf[...], preferred_element_type=F32)
-                gate, up = gu[:ff], gu[ff:]
-                hidden = gate * jax.nn.sigmoid(gate) * up
-                ombuf[:, pl.ds(HEAD_DIM, ff)] = hidden.T.astype(BF16)
+                up = jnp.dot(wall[pl.ds(3 * HEAD_DIM + ff, ff), :], atbuf[...], preferred_element_type=F32)
+                ombuf[:, pl.ds(HEAD_DIM, ff)] = (silu[...] * up).T.astype(BF16)
 
     tiles = width // OUT_TILE
 
-    def out_tiles(c, first, last):
-        om = ombuf[...]
-        for n in range(first, last):
+    def share_out(b, i):
+        @pl.when(b >= SLOTS)
+        def _():
+            pair_copy(b - SLOTS).wait_send()
+
+        om = ombuf[pl.ds(i * ROWS, ROWS), :]
+        for n in range(tiles):
             cols = pl.ds(n * OUT_TILE, OUT_TILE)
-            share = jnp.dot(om, wod[:, cols], preferred_element_type=F32).astype(BF16)
-            for i in (0, 1):
-                part[lax.rem(2 * c + i, SLOTS), :, cols] = share[i * ROWS:(i + 1) * ROWS]
-            early = tiles // 2
-            if n < early:
-                for r in range((early + n) * PAIR // tiles, (early + n + 1) * PAIR // tiles, 16):
+            part[lax.rem(b, SLOTS), :, cols] = jnp.dot(om, wod[:, cols], preferred_element_type=F32).astype(BF16)
+            if i == 0:
+                for r in range(n * PAIR // tiles, (n + 1) * PAIR // tiles, 16):
                     norm_rows(r)
             else:
-                late = width // LANES // (tiles - early)
-                for j in range((n - early) * late, (n - early + 1) * late):
+                for j in range(n * width // LANES // tiles, (n + 1) * width // LANES // tiles):
                     turn(j)
-
-    def out_a(c):
-        @pl.when(c == 0)
-        def _():
-            for cp in w_loads[5:]:
-                cp.wait()
-
-        @pl.when(c >= 2)
-        def _():
-            pair_copy(2 * c - 4).wait_send()
-            pair_copy(2 * c - 3).wait_send()
-
-        out_tiles(c, 0, tiles // 2)
-
-        @pl.when(c + 2 < npair)
-        def _():
-            for cp in x_load(c + 2, lax.rem(c, 2)):
-                cp.start()
-
-    def out_b(c):
-        out_tiles(c, tiles // 2, tiles)
-        pair_copy(2 * c).start()
-        pair_copy(2 * c + 1).start()
+        pair_copy(b).start()
 
     def add(dst, *srcs):
         total = dst[...].astype(F32)
@@ -401,25 +383,39 @@
 
     @pl.loop(0, nblk + LAG[-1])
     def _(t):
-        def run(group):
-            for n in group:
-                b = t - LAG[n - 1]
-
-                @pl.when((b >= 0) & (b < nblk))
-                def _(b=b, n=n):
-                    stages[n - 1](b)
-
-        def work(parity, piece):
-            @pl.when((t < nblk) & (lax.rem(t, 2) == parity))
+        even = lax.rem(t, 2) == 0
+
+        @pl.when(even & (t >= 2) & (t <= nblk))
+        def _():
+            share_out(t - 1, 1)
+
+        @pl.when(even & (t < nblk))
+        def _():
+            project(t // 2)
+            open_gate(t // 2)
+
+        @pl.when((t < nblk) & (lax.rem(t, 2) == 1))
+        def _():
+            c = t // 2
+            mix(c)
+
+            @pl.when(c + 1 < npair)
             def _():
-                piece(t // 2)
-
-        work(0, project)
-        work(1, out_a)
-        run(FIRST)
-        work(0, mix)
-        work(1, out_b)
-        run(SECOND)
+                wait_all(x_load(c + 1, lax.rem(c + 1, 2)))
+
+            share_out(t - 1, 0)
+
+            @pl.when(c + 2 < npair)
+            def _():
+                for cp in x_load(c + 2, lax.rem(c, 2)):
+                    cp.start()
+
+        for lag, stage in zip(LAG, stages):
+            b = t - lag
+
+            @pl.when((b >= 0) & (b < nblk))
+            def _(b=b, stage=stage):
+                stage(b)
 
     for b in range(nblk - SLOTS, nblk):
         pair_copy(b).wait_send()
@@ -468,6 +464,7 @@
                 pltpu.VMEM((width, PAIR), BF16),
                 pltpu.VMEM((16, width), F32),
                 pltpu.VMEM((HEAD_DIM, PAIR), BF16),
+                pltpu.VMEM((ff, PAIR), F32),
                 pltpu.VMEM((PAIR, HEAD_DIM + ff), BF16),
                 pltpu.VMEM((tokens, HEAD_DIM), BF16),
                 pltpu.VMEM((2, PAIR, HEAD_DIM), BF16),

time: 185 us -> 157 us (0.85)
  Pallas kernels: 176 us -> 148 us
    pallas_call x1, Pallas kernels: 176 us -> 148 us  [local_layer(): pl.pallas_call(functools.partial(layer_kernel, (tp_size, side, kv_heads))...]
where the time goes in v4:
time: 157 us
  Pallas kernels  148 us (94%)
  local copies, waits for them, and re-layouts  7.76 us (5%)
    pallas_call x1, Pallas kernels, local_layer(): pl.pallas_call(functools.partial(layer_kernel, (tp_size, side, kv_heads))...  148 us
    unnamed x7, local copies, waits for them, and re-layouts  7.76 us

profile of v4, /device:TPU:97, one launch (start us, length us, event | category | flops | bytes accessed | tf_op | source)
XLA Modules:
  0.0 156.8 jit_solution(12289331325427216978)
XLA Ops:
  0.6 148.4 %layer.1 = (bf16[2048,4096]{1,0:T(8,128)(2,1)S(1)}, bf16[2048,128]{1,0:T(8,128)(2,1)}, bf16[2048,128]{1,0:T(8,128)(2,1)}) custom-call(bf16[2048,4096]{1,0:T(8,128)(2,1)} %x_hbm.1, bf16[32,128]{1,0:T(8,128)(2,1)} %bitcast.9, f32[2,64,2048]{2,1,0:T(8,128)} %constant.2.clone.tab_hbm, bf16[4096,128]{1,0:T(8,128)(2,1)} %wq_hbm.1, bf16[4096,1024]{1,0:T(8,128)(2,1)} %wk_hbm.1, ...), custom_call_target="tpu_custom_call" | custom-call | tf_op jit(solution)/shard_map/layer/pallas_call | solution.py:450
  149.0 0.0 copy-start.1
  149.0 0.0 copy-start
  149.0 6.2 %copy.16 = bf16[2048,4096]{1,0:T(8,128)(2,1)} copy(bf16[2048,4096]{1,0:T(8,128)(2,1)S(1)} %get-tuple-element.9) | data formatting | bytes 33554432
  155.2 0.0 copy-done.1
  155.2 0.8 copy.17
  156.0 0.0 copy-done
  156.0 0.8 copy.18
Async XLA Ops:
  149.0 6.2 %copy-start.1 = (bf16[2048,128]{1,0:T(8,128)(2,1)S(1)}, bf16[2048,128]{1,0:T(8,128)(2,1)}, u32[]{:S(2)}) copy-start(bf16[2048,128]{1,0:T(8,128)(2,1)} %get-tuple-element.7) | copy-start | bytes 1572868
  149.0 7.0 %copy-start = (bf16[2048,128]{1,0:T(8,128)(2,1)S(1)}, bf16[2048,128]{1,0:T(8,128)(2,1)}, u32[]{:S(2)}) copy-start(bf16[2048,128]{1,0:T(8,128)(2,1)} %get-tuple-element.8) | copy-start | bytes 1572868

commit v5 on v4

--- a/solution.py
+++ b/solution.py
@@ -13,24 +13,22 @@
 NORM_EPS = 1e-5
 LANES = 128
 ROWS = 128
-PAIR = 2 * ROWS
 SLOTS = 2
 RING = 4
 KEYS = 512
 OUT_TILE = 512
-LAG = (2, 3, 4, 5, 6, 7, 8, 9, 10, 11)
+LAG = (1, 2, 3, 4, 5, 6, 7, 8, 9, 10)
 BF16 = jnp.bfloat16
 F32 = jnp.float32
 
 
 def layer_kernel(cfg, x_hbm, g_ref, tab_hbm, wq_hbm, wk_hbm, wv_hbm, wo_hbm, wg_hbm, wu_hbm, wd_hbm,
                  ybuf, k_hbm, v_hbm,
-                 wqkv, wall, wod, xbuf, tabs, abuf, atbuf, gbuf, qtbuf, silu, ombuf, kbuf, vbuf, vtbuf, part, quart, r1, r2, r3, r4, xres,
+                 wall, wgu, wod, xbuf, tabs, abuf, gbuf, ombuf, kbuf, vbuf, part, quart, r1, r2, r3, r4, xres,
                  wsem, xsem, ressem, kvsem, pair_send, pair_recv, ssem, rsem, gpair_send, gpair_recv):
     tokens, width = x_hbm.shape
     tp, side, kv_heads = cfg[:3]
     nblk = tokens // ROWS
-    npair = tokens // PAIR
     half = width // 2
     quarter = half // 2
     cw = quarter // side
@@ -65,21 +63,22 @@
     mine0 = core * half
     res_col = [pl.multiple_of(mine0 + ab * quarter + pos[ab] * cw, cw) for ab in (0, 1)]
 
-    def x_load(c, slot):
-        rows = pl.ds(pl.multiple_of(c * PAIR, PAIR), PAIR)
+    def x_load(b):
+        rows = pl.ds(pl.multiple_of(b * ROWS, ROWS), ROWS)
+        slot = lax.rem(b, 2)
         return (pltpu.make_async_copy(x_hbm.at[rows], xbuf, xsem.at[slot, 0]),
-                pltpu.make_async_copy(tab_hbm.at[:, :, rows], tabs.at[slot], xsem.at[slot, 1]))
+                pltpu.make_async_copy(tab_hbm.at[:, rows], tabs.at[slot], xsem.at[slot, 1]))
 
     w_loads = (
-        pltpu.make_async_copy(wq_hbm, wqkv.at[0], wsem.at[0]),
-        pltpu.make_async_copy(wk_hbm.at[:, kcol], wqkv.at[1], wsem.at[1]),
-        pltpu.make_async_copy(wv_hbm.at[:, kcol], wqkv.at[2], wsem.at[2]),
-        pltpu.make_async_copy(wg_hbm, wall.at[pl.ds(3 * HEAD_DIM, ff)], wsem.at[3]),
-        pltpu.make_async_copy(wu_hbm, wall.at[pl.ds(3 * HEAD_DIM + ff, ff)], wsem.at[4]),
+        pltpu.make_async_copy(wg_hbm, wgu.at[pl.ds(0, ff)], wsem.at[0]),
+        pltpu.make_async_copy(wu_hbm, wgu.at[pl.ds(ff, ff)], wsem.at[1]),
+        pltpu.make_async_copy(wq_hbm, wall.at[:, pl.ds(0, HEAD_DIM)], wsem.at[2]),
+        pltpu.make_async_copy(wk_hbm.at[:, kcol], wall.at[:, pl.ds(HEAD_DIM, HEAD_DIM)], wsem.at[3]),
+        pltpu.make_async_copy(wv_hbm.at[:, kcol], wall.at[:, pl.ds(2 * HEAD_DIM, HEAD_DIM)], wsem.at[4]),
         pltpu.make_async_copy(wo_hbm, wod.at[pl.ds(0, HEAD_DIM)], wsem.at[5]),
         pltpu.make_async_copy(wd_hbm, wod.at[pl.ds(HEAD_DIM, ff)], wsem.at[6]),
     )
-    for c in x_load(0, 0):
+    for c in x_load(0):
         c.start()
     for c in w_loads:
         c.start()
@@ -87,7 +86,7 @@
     for c in res_loads:
         c.start()
     kbuf[...] = jnp.zeros_like(kbuf)
-    vtbuf[...] = jnp.zeros_like(vtbuf)
+    vbuf[...] = jnp.zeros_like(vbuf)
 
     def pair_copy(b):
         col = pl.multiple_of((1 - core) * half, half)
@@ -177,11 +176,11 @@
         for cp in copies:
             cp.wait()
 
-    def kv_store(c):
-        rows = pl.ds(pl.multiple_of(c * PAIR, PAIR), PAIR)
-        slot = lax.rem(c, 2)
+    def kv_store(b):
+        rows = yrows(b)
+        slot = lax.rem(b, 2)
         return (pltpu.make_async_copy(kbuf.at[rows], k_hbm.at[rows], kvsem.at[slot, 0]),
-                pltpu.make_async_copy(vbuf.at[slot], v_hbm.at[rows], kvsem.at[slot, 1]))
+                pltpu.make_async_copy(vbuf.at[rows], v_hbm.at[rows], kvsem.at[slot, 1]))
 
     def issue(send, b):
         @pl.when(b >= 2)
@@ -190,19 +189,19 @@
 
         both(lambda ab, d: send(b, ab, d).start())
 
-    def attend(q_t, c, keys):
-        s = jnp.dot(kbuf[pl.ds(0, keys), :], q_t, preferred_element_type=F32)
+    def attend(q, b, keys):
+        s = lax.dot_general(q, kbuf[pl.ds(0, keys), :], (((1,), (1,)), ((), ())), preferred_element_type=F32)
         edge = keys - KEYS
-        tail = s[edge:]
-        kpos = edge + lax.broadcasted_iota(jnp.int32, tail.shape, 0)
-        qpos = c * PAIR + lax.broadcasted_iota(jnp.int32, tail.shape, 1)
+        tail = s[:, edge:]
+        qpos = b * ROWS + lax.broadcasted_iota(jnp.int32, tail.shape, 0)
+        kpos = edge + lax.broadcasted_iota(jnp.int32, tail.shape, 1)
         tail = jnp.where(kpos <= qpos, tail, -1e30)
-        s = jnp.concatenate([s[:edge], tail], axis=0) if edge else tail
-        top = jnp.max(s, axis=0, keepdims=True)
+        s = jnp.concatenate([s[:, :edge], tail], axis=1) if edge else tail
+        top = jnp.max(s, axis=-1, keepdims=True)
         e = jnp.exp2((s - top) * (math.log2(math.e) / math.sqrt(HEAD_DIM)))
-        probs = (e * (1.0 / jnp.sum(e, axis=0, keepdims=True))).astype(BF16)
-        o_t = jnp.dot(vtbuf[:, pl.ds(0, keys)], probs, preferred_element_type=F32)
-        ombuf[:, pl.ds(0, HEAD_DIM)] = o_t.T.astype(BF16)
+        probs = (e * (1.0 / jnp.sum(e, axis=-1, keepdims=True))).astype(BF16)
+        o = jnp.dot(probs, vbuf[pl.ds(0, keys), :], preferred_element_type=F32)
+        ombuf[:, pl.ds(0, HEAD_DIM)] = o.astype(BF16)
 
     def norm_rows(r):
         rows = pl.ds(r, 16)
@@ -216,92 +215,83 @@
             cols = pl.ds(j * LANES, LANES)
             abuf[rows, cols] = (xbuf[rows, cols].astype(F32) * inv * gbuf[:, cols]).astype(BF16)
 
-    def turn(j):
-        cols = pl.ds(j * LANES, LANES)
-        atbuf[cols, :] = abuf[:, cols].T
-
-    def first_norm():
+    def prepare():
         for j in range(width // LANES):
             gbuf[:, j * LANES:(j + 1) * LANES] = jnp.broadcast_to(g_ref[j:j + 1, :].astype(F32), (16, LANES))
-
-        for cp in x_load(0, 0):
-            cp.wait()
-        @pl.loop(0, PAIR // 16)
+        wait_all(x_load(0))
+
+        @pl.loop(0, ROWS // 16)
         def _(i):
             norm_rows(pl.multiple_of(i * 16, 16))
 
-        for cp in x_load(1, 1):
+        for cp in x_load(1):
             cp.start()
-        for j in range(width // LANES):
-            turn(j)
-        for cp in w_loads[:3]:
-            cp.wait()
-        for r in range(0, width, 512):
-            for n in range(3):
-                wall[pl.ds(n * HEAD_DIM, HEAD_DIM), pl.ds(r, 512)] = wqkv[n, pl.ds(r, 512), :].T
-
-    def project(c):
-        slot = lax.rem(c, 2)
-        qkv = jnp.dot(wall[pl.ds(0, 3 * HEAD_DIM), :], atbuf[...], preferred_element_type=F32)
+
+        wait_all(w_loads[:2])
+
+        @pl.loop(0, width // KEYS)
+        def _(i):
+            rows = pl.ds(pl.multiple_of(i * KEYS, KEYS), KEYS)
+            for m in range(0, 2 * ff, LANES):
+                wall[rows, pl.ds(3 * HEAD_DIM + m, LANES)] = wgu[pl.ds(m, LANES), rows].T
+
+        wait_all(w_loads[2:5])
+
+    tiles = width // OUT_TILE
+
+    def compute(b):
+        slot = lax.rem(b, 2)
+        proj = jnp.dot(abuf[...], wall[...], preferred_element_type=F32)
         cos_t = tabs[slot, 0]
         sin_t = tabs[slot, 1]
 
         def rope(z):
-            lo, hi = z[:HEAD_DIM // 2], z[HEAD_DIM // 2:]
-            return jnp.concatenate([lo * cos_t - hi * sin_t, hi * cos_t + lo * sin_t], axis=0)
-
-        qtbuf[...] = rope(qkv[:HEAD_DIM]).astype(BF16)
-        rows = pl.ds(pl.multiple_of(c * PAIR, PAIR), PAIR)
-        kbuf[rows, :] = rope(qkv[HEAD_DIM:2 * HEAD_DIM]).T.astype(BF16)
-        v_t = qkv[2 * HEAD_DIM:]
-        vtbuf[:, rows] = v_t.astype(BF16)
-        @pl.when(c >= 2)
-        def _():
-            for cp in kv_store(c - 2):
-                cp.wait()
-
-        vbuf[slot] = v_t.T.astype(BF16)
-        for cp in kv_store(c):
+            return (z * cos_t + pltpu.roll(z, HEAD_DIM // 2, 1) * sin_t).astype(BF16)
+
+        q = rope(proj[:, :HEAD_DIM])
+        rows = yrows(b)
+        kbuf[rows, :] = rope(proj[:, HEAD_DIM:2 * HEAD_DIM])
+        vbuf[rows, :] = proj[:, 2 * HEAD_DIM:3 * HEAD_DIM].astype(BF16)
+        gate = proj[:, 3 * HEAD_DIM:3 * HEAD_DIM + ff]
+        up = proj[:, 3 * HEAD_DIM + ff:]
+        ombuf[:, pl.ds(HEAD_DIM, ff)] = (gate * jax.nn.sigmoid(gate) * up).astype(BF16)
+
+        @pl.when(b >= 2)
+        def _():
+            wait_all(kv_store(b - 2))
+
+        for cp in kv_store(b):
             cp.start()
 
-    def open_gate(c):
-        @pl.when(c == 0)
-        def _():
-            wait_all(w_loads[3:4])
-
-        gate = jnp.dot(wall[pl.ds(3 * HEAD_DIM, ff), :], atbuf[...], preferred_element_type=F32)
-        silu[...] = gate * jax.nn.sigmoid(gate)
-
-    def mix(c):
-        @pl.when(c == 0)
-        def _():
-            wait_all(w_loads[4:])
-
         for n in range(tokens // KEYS):
-            @pl.when(c * PAIR // KEYS == n)
+            @pl.when(b * ROWS // KEYS == n)
             def _(n=n):
-                attend(qtbuf[...], c, (n + 1) * KEYS)
-                up = jnp.dot(wall[pl.ds(3 * HEAD_DIM + ff, ff), :], atbuf[...], preferred_element_type=F32)
-                ombuf[:, pl.ds(HEAD_DIM, ff)] = (silu[...] * up).T.astype(BF16)
-
-    tiles = width // OUT_TILE
-
-    def share_out(b, i):
+                attend(q, b, (n + 1) * KEYS)
+
+        @pl.when(b == 0)
+        def _():
+            wait_all(w_loads[5:])
+
         @pl.when(b >= SLOTS)
         def _():
             pair_copy(b - SLOTS).wait_send()
 
-        om = ombuf[pl.ds(i * ROWS, ROWS), :]
+        @pl.when(b + 1 < nblk)
+        def _():
+            wait_all(x_load(b + 1))
+
+        om = ombuf[...]
         for n in range(tiles):
             cols = pl.ds(n * OUT_TILE, OUT_TILE)
-            part[lax.rem(b, SLOTS), :, cols] = jnp.dot(om, wod[:, cols], preferred_element_type=F32).astype(BF16)
-            if i == 0:
-                for r in range(n * PAIR // tiles, (n + 1) * PAIR // tiles, 16):
-                    norm_rows(r)
-            else:
-                for j in range(n * width // LANES // tiles, (n + 1) * width // LANES // tiles):
-                    turn(j)
+            part[slot, :, cols] = jnp.dot(om, wod[:, cols], preferred_element_type=F32).astype(BF16)
+            for r in range(n * ROWS // tiles, (n + 1) * ROWS // tiles, 16):
+                norm_rows(r)
         pair_copy(b).start()
+
+        @pl.when(b + 2 < nblk)
+        def _():
+            for cp in x_load(b + 2):
+                cp.start()
 
     def add(dst, *srcs):
         total = dst[...].astype(F32)
@@ -378,37 +368,14 @@
 
     stages = (stage1, stage2, stage3, stage4, stage5, stage6, stage7, stage8, stage9, stage10)
 
-    first_norm()
+    prepare()
     pl.semaphore_wait(barrier, 5)
 
     @pl.loop(0, nblk + LAG[-1])
     def _(t):
-        even = lax.rem(t, 2) == 0
-
-        @pl.when(even & (t >= 2) & (t <= nblk))
-        def _():
-            share_out(t - 1, 1)
-
-        @pl.when(even & (t < nblk))
-        def _():
-            project(t // 2)
-            open_gate(t // 2)
-
-        @pl.when((t < nblk) & (lax.rem(t, 2) == 1))
-        def _():
-            c = t // 2
-            mix(c)
-
-            @pl.when(c + 1 < npair)
-            def _():
-                wait_all(x_load(c + 1, lax.rem(c + 1, 2)))
-
-            share_out(t - 1, 0)
-
-            @pl.when(c + 2 < npair)
-            def _():
-                for cp in x_load(c + 2, lax.rem(c, 2)):
-                    cp.start()
+        @pl.when(t < nblk)
+        def _():
+            compute(t)
 
         for lag, stage in zip(LAG, stages):
             b = t - lag
@@ -423,15 +390,15 @@
         for send in sends:
             both(lambda ab, d: send(b, ab, d).wait_send())
         gpair(b, core).wait_send()
-    for c in range(nblk // 2 - 2, nblk // 2):
-        for cp in kv_store(c):
-            cp.wait()
+    for b in range(nblk - 2, nblk):
+        wait_all(kv_store(b))
 
 
 def rope_tables(tokens):
     inv_freq = np.float32(ROPE_BASE) ** (-np.arange(0, HEAD_DIM, 2, dtype=np.float32) / np.float32(HEAD_DIM))
     angles = np.arange(tokens, dtype=np.float32)[:, None] * inv_freq[None, :]
-    return np.stack([np.cos(angles).T, np.sin(angles).T])
+    cos_half, sin_half = np.cos(angles), np.sin(angles)
+    return np.stack([np.concatenate([cos_half, cos_half], axis=1), np.concatenate([-sin_half, sin_half], axis=1)])
 
 
 def solution(mesh):
@@ -455,20 +422,16 @@
             in_specs=[any_spec, pl.BlockSpec(memory_space=pltpu.VMEM)] + [any_spec] * 8,
             out_specs=(pl.BlockSpec(memory_space=pltpu.VMEM), any_spec, any_spec),
             scratch_shapes=[
-                pltpu.VMEM((3, width, HEAD_DIM), BF16),
-                pltpu.VMEM((3 * HEAD_DIM + 2 * ff, width), BF16),
+                pltpu.VMEM((width, 3 * HEAD_DIM + 2 * ff), BF16),
+                pltpu.VMEM((2 * ff, width), BF16),
                 pltpu.VMEM((HEAD_DIM + ff, width), BF16),
-                pltpu.VMEM((PAIR, width), BF16),
-                pltpu.VMEM((2, 2, HEAD_DIM // 2, PAIR), F32),
-                pltpu.VMEM((PAIR, width), BF16),
-                pltpu.VMEM((width, PAIR), BF16),
+                pltpu.VMEM((ROWS, width), BF16),
+                pltpu.VMEM((2, 2, ROWS, HEAD_DIM), F32),
+                pltpu.VMEM((ROWS, width), BF16),
                 pltpu.VMEM((16, width), F32),
-                pltpu.VMEM((HEAD_DIM, PAIR), BF16),
-                pltpu.VMEM((ff, PAIR), F32),
-                pltpu.VMEM((PAIR, HEAD_DIM + ff), BF16),
+                pltpu.VMEM((ROWS, HEAD_DIM + ff), BF16),
                 pltpu.VMEM((tokens, HEAD_DIM), BF16),
-                pltpu.VMEM((2, PAIR, HEAD_DIM), BF16),
-                pltpu.VMEM((HEAD_DIM, tokens), BF16),
+                pltpu.VMEM((tokens, HEAD_DIM), BF16),
                 pltpu.VMEM((SLOTS, ROWS, width), BF16),
                 pltpu.VMEM((nblk, ROWS, half), BF16),
                 pltpu.VMEM((RING, 2, 2, ROWS, cw // 2), BF16),

time: 157 us -> 143 us (0.911)
  Pallas kernels: 148 us -> 134 us
    pallas_call x1, Pallas kernels: 148 us -> 134 us  [local_layer(): pl.pallas_call(functools.partial(layer_kernel, (tp_size, side, kv_heads))...]
where the time goes in v5:
time: 143 us; the launch traced here: 142 us
  Pallas kernels  134 us (94%)
  local copies, waits for them, and re-layouts  7.76 us (5%)
    pallas_call x1, Pallas kernels, local_layer(): pl.pallas_call(functools.partial(layer_kernel, (tp_size, side, kv_heads))...  134 us
    unnamed x7, local copies, waits for them, and re-layouts  7.76 us

profile of v5, /device:TPU:97, one launch (start us, length us, event | category | flops | bytes accessed | tf_op | source)
XLA Modules:
  0.0 142.5 jit_solution(1899050049505950278)
XLA Ops:
  0.6 134.0 %layer.1 = (bf16[2048,4096]{1,0:T(8,128)(2,1)S(1)}, bf16[2048,128]{1,0:T(8,128)(2,1)}, bf16[2048,128]{1,0:T(8,128)(2,1)}) custom-call(bf16[2048,4096]{1,0:T(8,128)(2,1)} %x_hbm.1, bf16[32,128]{1,0:T(8,128)(2,1)} %bitcast.9, f32[2,2048,128]{2,1,0:T(8,128)} %constant.2.clone.tab_hbm, bf16[4096,128]{1,0:T(8,128)(2,1)} %wq_hbm.1, bf16[4096,1024]{1,0:T(8,128)(2,1)} %wk_hbm.1, ...), custom_call_target="tpu_custom_call" | custom-call | tf_op jit(solution)/shard_map/layer/pallas_call | solution.py:417
  134.7 0.0 copy-start.1
  134.7 0.0 copy-start
  134.7 6.2 %copy.16 = bf16[2048,4096]{1,0:T(8,128)(2,1)} copy(bf16[2048,4096]{1,0:T(8,128)(2,1)S(1)} %get-tuple-element.9) | data formatting | bytes 33554432
  140.9 0.0 copy-done.1
  140.9 0.8 copy.17
  141.7 0.0 copy-done
  141.7 0.8 copy.18
Async XLA Ops:
  134.7 6.2 %copy-start.1 = (bf16[2048,128]{1,0:T(8,128)(2,1)S(1)}, bf16[2048,128]{1,0:T(8,128)(2,1)}, u32[]{:S(2)}) copy-start(bf16[2048,128]{1,0:T(8,128)(2,1)} %get-tuple-element.7) | copy-start | bytes 1572868
  134.7 7.0 %copy-start = (bf16[2048,128]{1,0:T(8,128)(2,1)S(1)}, bf16[2048,128]{1,0:T(8,128)(2,1)}, u32[]{:S(2)}) copy-start(bf16[2048,128]{1,0:T(8,128)(2,1)} %get-tuple-element.8) | copy-start | bytes 1572868

commit v6 on v5

--- a/solution.py
+++ b/solution.py
@@ -18,14 +18,16 @@
 KEYS = 512
 OUT_TILE = 512
 LAG = (1, 2, 3, 4, 5, 6, 7, 8, 9, 10)
+FIRST = (1, 2, 3, 4, 5)
+SECOND = (6, 7, 8, 9, 10)
 BF16 = jnp.bfloat16
 F32 = jnp.float32
 
 
 def layer_kernel(cfg, x_hbm, g_ref, tab_hbm, wq_hbm, wk_hbm, wv_hbm, wo_hbm, wg_hbm, wu_hbm, wd_hbm,
-                 ybuf, k_hbm, v_hbm,
-                 wall, wgu, wod, xbuf, tabs, abuf, gbuf, ombuf, kbuf, vbuf, part, quart, r1, r2, r3, r4, xres,
-                 wsem, xsem, ressem, kvsem, pair_send, pair_recv, ssem, rsem, gpair_send, gpair_recv):
+                 ybuf, kbuf, vbuf,
+                 wall, wgu, wod, xbuf, tabs, abuf, gbuf, ombuf, part, quart, r1, r2, r3, r4, xres,
+                 wsem, xsem, ressem, pair_send, pair_recv, ssem, rsem, gpair_send, gpair_recv):
     tokens, width = x_hbm.shape
     tp, side, kv_heads = cfg[:3]
     nblk = tokens // ROWS
@@ -176,12 +178,6 @@
         for cp in copies:
             cp.wait()
 
-    def kv_store(b):
-        rows = yrows(b)
-        slot = lax.rem(b, 2)
-        return (pltpu.make_async_copy(kbuf.at[rows], k_hbm.at[rows], kvsem.at[slot, 0]),
-                pltpu.make_async_copy(vbuf.at[rows], v_hbm.at[rows], kvsem.at[slot, 1]))
-
     def issue(send, b):
         @pl.when(b >= 2)
         def _():
@@ -256,17 +252,13 @@
         up = proj[:, 3 * HEAD_DIM + ff:]
         ombuf[:, pl.ds(HEAD_DIM, ff)] = (gate * jax.nn.sigmoid(gate) * up).astype(BF16)
 
-        @pl.when(b >= 2)
-        def _():
-            wait_all(kv_store(b - 2))
-
-        for cp in kv_store(b):
-            cp.start()
-
         for n in range(tokens // KEYS):
             @pl.when(b * ROWS // KEYS == n)
             def _(n=n):
                 attend(q, b, (n + 1) * KEYS)
+
+    def finish(b):
+        slot = lax.rem(b, 2)
 
         @pl.when(b == 0)
         def _():
@@ -373,16 +365,25 @@
 
     @pl.loop(0, nblk + LAG[-1])
     def _(t):
+        def run(group):
+            for n in group:
+                b = t - LAG[n - 1]
+
+                @pl.when((b >= 0) & (b < nblk))
+                def _(b=b, n=n):
+                    stages[n - 1](b)
+
         @pl.when(t < nblk)
         def _():
             compute(t)
 
-        for lag, stage in zip(LAG, stages):
-            b = t - lag
-
-            @pl.when((b >= 0) & (b < nblk))
-            def _(b=b, stage=stage):
-                stage(b)
+        run(FIRST)
+
+        @pl.when(t < nblk)
+        def _():
+            finish(t)
+
+        run(SECOND)
 
     for b in range(nblk - SLOTS, nblk):
         pair_copy(b).wait_send()
@@ -390,8 +391,19 @@
         for send in sends:
             both(lambda ab, d: send(b, ab, d).wait_send())
         gpair(b, core).wait_send()
-    for b in range(nblk - 2, nblk):
-        wait_all(kv_store(b))
+
+
+def store_kernel(y_ref, k_ref, v_ref, y_hbm, k_hbm, v_hbm, sems):
+    pieces = sems.shape[0] - 2
+    rows = y_ref.shape[0] // pieces
+    copies = [pltpu.make_async_copy(y_ref.at[pl.ds(i * rows, rows)], y_hbm.at[pl.ds(i * rows, rows)], sems.at[i])
+              for i in range(pieces)]
+    copies.append(pltpu.make_async_copy(k_ref, k_hbm, sems.at[pieces]))
+    copies.append(pltpu.make_async_copy(v_ref, v_hbm, sems.at[pieces + 1]))
+    for cp in copies:
+        cp.start()
+    for cp in copies:
+        cp.wait()
 
 
 def rope_tables(tokens):
@@ -417,10 +429,10 @@
         y, k, v = pl.pallas_call(
             functools.partial(layer_kernel, (tp_size, side, kv_heads)),
             out_shape=(pltpu.VMEM((tokens, width), BF16),
-                       jax.ShapeDtypeStruct((tokens, HEAD_DIM), BF16),
-                       jax.ShapeDtypeStruct((tokens, HEAD_DIM), BF16)),
+                       pltpu.VMEM((tokens, HEAD_DIM), BF16),
+                       pltpu.VMEM((tokens, HEAD_DIM), BF16)),
             in_specs=[any_spec, pl.BlockSpec(memory_space=pltpu.VMEM)] + [any_spec] * 8,
-            out_specs=(pl.BlockSpec(memory_space=pltpu.VMEM), any_spec, any_spec),
+            out_specs=(pl.BlockSpec(memory_space=pltpu.VMEM),) * 3,
             scratch_shapes=[
                 pltpu.VMEM((width, 3 * HEAD_DIM + 2 * ff), BF16),
                 pltpu.VMEM((2 * ff, width), BF16),
@@ -430,8 +442,6 @@
                 pltpu.VMEM((ROWS, width), BF16),
                 pltpu.VMEM((16, width), F32),
                 pltpu.VMEM((ROWS, HEAD_DIM + ff), BF16),
-                pltpu.VMEM((tokens, HEAD_DIM), BF16),
-                pltpu.VMEM((tokens, HEAD_DIM), BF16),
                 pltpu.VMEM((SLOTS, ROWS, width), BF16),
                 pltpu.VMEM((nblk, ROWS, half), BF16),
                 pltpu.VMEM((RING, 2, 2, ROWS, cw // 2), BF16),
@@ -442,7 +452,6 @@
                 pltpu.SemaphoreType.DMA((7,)),
                 pltpu.SemaphoreType.DMA((2, 2)),
                 pltpu.SemaphoreType.DMA((2,)),
-                pltpu.SemaphoreType.DMA((2, 2)),
                 pltpu.SemaphoreType.DMA((SLOTS,)),
                 pltpu.SemaphoreType.DMA((nblk,)),
                 pltpu.SemaphoreType.DMA((8, 2, 2, 2)),
@@ -450,9 +459,20 @@
                 pltpu.SemaphoreType.DMA((2,)),
                 pltpu.SemaphoreType.DMA((nblk,)),
             ],
-            compiler_params=pltpu.CompilerParams(collective_id=0, has_side_effects=True, vmem_limit_bytes=47 * 1024 * 1024),
+            compiler_params=pltpu.CompilerParams(collective_id=0, has_side_effects=True, vmem_limit_bytes=46 * 1024 * 1024),
             name="layer",
         )(x_in, g_norm.reshape(width // LANES, LANES), jnp.asarray(rope_tables(tokens)), w_q, w_k, w_v, w_o, w_gate.T, w_up.T, w_down)
+        y, k, v = pl.pallas_call(
+            store_kernel,
+            out_shape=(jax.ShapeDtypeStruct((tokens, width), BF16),
+                       jax.ShapeDtypeStruct((tokens, HEAD_DIM), BF16),
+                       jax.ShapeDtypeStruct((tokens, HEAD_DIM), BF16)),
+            in_specs=[any_spec] * 3,
+            out_specs=(any_spec,) * 3,
+            scratch_shapes=[pltpu.SemaphoreType.DMA((10,))],
+            compiler_params=pltpu.CompilerParams(vmem_limit_bytes=1024 * 1024),
+            name="store",
+        )(y, k, v)
         return y, k.reshape(tokens, 1, HEAD_DIM), v.reshape(tokens, 1, HEAD_DIM)
 
     return jax.shard_map(local_layer, mesh=mesh, in_specs=(P('dp', None), P(None), P(None, 'tp'), P(None, None), P(None, None), P('tp', None), P(None, 'tp'), P(None, 'tp'), P('tp', None)), out_specs=(P('dp', None), P('dp', 'tp', None), P('dp', 'tp', None)), check_vma=False)

time: 143 us -> 138 us (0.965)
  local copies, waits for them, and re-layouts: 7.76 us -> 0 us
  Pallas kernels: 134 us -> 137 us
    unnamed x7 -> x0, local copies, waits for them, and re-layouts: 7.76 us -> none
    pallas_call x0 -> x1, Pallas kernels: none -> 6.21 us  [local_layer(): pl.pallas_call(store_kernel, out_shape=(jax.ShapeDtypeStruct((tokens, wid...]
    pallas_call x1, Pallas kernels: 134 us -> 131 us  [local_layer(): pl.pallas_call(functools.partial(layer_kernel, (tp_size, side, kv_heads))...]
where the time goes in v6:
time: 138 us
  Pallas kernels  137 us (99%)
    pallas_call x1, Pallas kernels, local_layer(): pl.pallas_call(functools.partial(layer_kernel, (tp_size, side, kv_heads))...  131 us
    pallas_call x1, Pallas kernels, local_layer(): pl.pallas_call(store_kernel, out_shape=(jax.ShapeDtypeStruct((tokens, wid...  6.21 us

profile of v6, /device:TPU:97, one launch (start us, length us, event | category | flops | bytes accessed | tf_op | source)
XLA Modules:
  0.0 138.1 jit_solution(6337394453002705608)
XLA Ops:
  0.6 131.3 %layer.1 = (bf16[2048,4096]{1,0:T(8,128)(2,1)S(1)}, bf16[2048,128]{1,0:T(8,128)(2,1)S(1)}, bf16[2048,128]{1,0:T(8,128)(2,1)S(1)}) custom-call(bf16[2048,4096]{1,0:T(8,128)(2,1)} %x_hbm.1, bf16[32,128]{1,0:T(8,128)(2,1)} %bitcast.7, f32[2,2048,128]{2,1,0:T(8,128)} %constant.2.clone.tab_hbm, bf16[4096,128]{1,0:T(8,128)(2,1)} %wq_hbm.1, ...), custom_call_target="tpu_custom_call" | custom-call | tf_op jit(solution)/shard_map/layer/pallas_call | solution.py:429
  131.9 6.2 %store.1 = (bf16[2048,4096]{1,0:T(8,128)(2,1)}, bf16[2048,128]{1,0:T(8,128)(2,1)}, bf16[2048,128]{1,0:T(8,128)(2,1)}) custom-call(bf16[2048,4096]{1,0:T(8,128)(2,1)S(1)} %get-tuple-element.9.y_ref, bf16[2048,128]{1,0:T(8,128)(2,1)S(1)} %get-tuple-element.10.k_ref, bf16[2048,128]{1,0:T(8,128)(2,1)S(1)} %get-tuple-element.11.v_ref), custom_call_target="tpu_custom_call" | custom-call | tf_op jit(solution)/shard_map/store/pallas_call | solution.py:465

commit v7 on v6

--- a/solution.py
+++ b/solution.py
@@ -17,7 +17,7 @@
 RING = 4
 KEYS = 512
 OUT_TILE = 512
-LAG = (1, 2, 3, 4, 5, 6, 7, 8, 9, 10)
+LAG = (1, 2, 3, 4, 5, 6, 7, 9, 11, 12)
 FIRST = (1, 2, 3, 4, 5)
 SECOND = (6, 7, 8, 9, 10)
 BF16 = jnp.bfloat16
@@ -223,13 +223,15 @@
         for cp in x_load(1):
             cp.start()
 
-        wait_all(w_loads[:2])
-
-        @pl.loop(0, width // KEYS)
-        def _(i):
-            rows = pl.ds(pl.multiple_of(i * KEYS, KEYS), KEYS)
-            for m in range(0, 2 * ff, LANES):
-                wall[rows, pl.ds(3 * HEAD_DIM + m, LANES)] = wgu[pl.ds(m, LANES), rows].T
+        split = ff // LANES * LANES
+        for first, last, load in ((0, split, 0), (split, 2 * ff, 1)):
+            wait_all(w_loads[load:load + 1])
+
+            @pl.loop(0, width // KEYS)
+            def _(i, first=first, last=last):
+                rows = pl.ds(pl.multiple_of(i * KEYS, KEYS), KEYS)
+                for m in range(first, last, LANES):
+                    wall[rows, pl.ds(3 * HEAD_DIM + m, LANES)] = wgu[pl.ds(m, LANES), rows].T
 
         wait_all(w_loads[2:5])
 
@@ -275,9 +277,9 @@
         om = ombuf[...]
         for n in range(tiles):
             cols = pl.ds(n * OUT_TILE, OUT_TILE)
-            part[slot, :, cols] = jnp.dot(om, wod[:, cols], preferred_element_type=F32).astype(BF16)
             for r in range(n * ROWS // tiles, (n + 1) * ROWS // tiles, 16):
                 norm_rows(r)
+            part[slot, :, cols] = jnp.dot(om, wod[:, cols], preferred_element_type=F32).astype(BF16)
         pair_copy(b).start()
 
         @pl.when(b + 2 < nblk)
@@ -286,6 +288,9 @@
                 cp.start()
 
     def add(dst, *srcs):
+        if len(srcs) == 1:
+            dst[...] = dst[...] + srcs[0][...]
+            return
         total = dst[...].astype(F32)
         for s in srcs:
             total = total + s[...].astype(F32)

time: 138 us -> 138 us (level)
  no operation moved by 1% of the time
where the time goes in v7:
time: 138 us
  Pallas kernels  137 us (99%)
    pallas_call x1, Pallas kernels, local_layer(): pl.pallas_call(functools.partial(layer_kernel, (tp_size, side, kv_heads))...  131 us
    pallas_call x1, Pallas kernels, local_layer(): pl.pallas_call(store_kernel, out_shape=(jax.ShapeDtypeStruct((tokens, wid...  6.21 us

profile of v7, /device:TPU:97, one launch (start us, length us, event | category | flops | bytes accessed | tf_op | source)
XLA Modules:
  0.0 138.0 jit_solution(1107262054338042891)
XLA Ops:
  0.6 131.2 %layer.1 = (bf16[2048,4096]{1,0:T(8,128)(2,1)S(1)}, bf16[2048,128]{1,0:T(8,128)(2,1)S(1)}, bf16[2048,128]{1,0:T(8,128)(2,1)S(1)}) custom-call(bf16[2048,4096]{1,0:T(8,128)(2,1)} %x_hbm.1, bf16[32,128]{1,0:T(8,128)(2,1)} %bitcast.7, f32[2,2048,128]{2,1,0:T(8,128)} %constant.2.clone.tab_hbm, bf16[4096,128]{1,0:T(8,128)(2,1)} %wq_hbm.1, ...), custom_call_target="tpu_custom_call" | custom-call | tf_op jit(solution)/shard_map/layer/pallas_call | solution.py:434
  131.8 6.2 %store.1 = (bf16[2048,4096]{1,0:T(8,128)(2,1)}, bf16[2048,128]{1,0:T(8,128)(2,1)}, bf16[2048,128]{1,0:T(8,128)(2,1)}) custom-call(bf16[2048,4096]{1,0:T(8,128)(2,1)S(1)} %get-tuple-element.9.y_ref, bf16[2048,128]{1,0:T(8,128)(2,1)S(1)} %get-tuple-element.10.k_ref, bf16[2048,128]{1,0:T(8,128)(2,1)S(1)} %get-tuple-element.11.v_ref), custom_call_target="tpu_custom_call" | custom-call | tf_op jit(solution)/shard_map/store/pallas_call | solution.py:470

commit v8 on v7

--- a/solution.py
+++ b/solution.py
@@ -17,9 +17,9 @@
 RING = 4
 KEYS = 512
 OUT_TILE = 512
-LAG = (1, 2, 3, 4, 5, 6, 7, 9, 11, 12)
-FIRST = (1, 2, 3, 4, 5)
-SECOND = (6, 7, 8, 9, 10)
+LAG = (1, 2, 3, 4, 5, 6, 7, 8, 9, 10)
+FIRST = (1, 2, 3)
+SECOND = (4, 5, 6, 7, 8, 9, 10)
 BF16 = jnp.bfloat16
 F32 = jnp.float32
 

time: 138 us -> 138 us (level)
  no operation moved by 1% of the time
where the time goes in v8:
time: 138 us
  Pallas kernels  138 us (100%)
    pallas_call x1, Pallas kernels, local_layer(): pl.pallas_call(functools.partial(layer_kernel, (tp_size, side, kv_heads))...  131 us
    pallas_call x1, Pallas kernels, local_layer(): pl.pallas_call(store_kernel, out_shape=(jax.ShapeDtypeStruct((tokens, wid...  6.21 us

profile of v8, /device:TPU:97, one launch (start us, length us, event | category | flops | bytes accessed | tf_op | source)
XLA Modules:
  0.0 138.1 jit_solution(12911755384999962770)
XLA Ops:
  0.6 131.3 %layer.1 = (bf16[2048,4096]{1,0:T(8,128)(2,1)S(1)}, bf16[2048,128]{1,0:T(8,128)(2,1)S(1)}, bf16[2048,128]{1,0:T(8,128)(2,1)S(1)}) custom-call(bf16[2048,4096]{1,0:T(8,128)(2,1)} %x_hbm.1, bf16[32,128]{1,0:T(8,128)(2,1)} %bitcast.7, f32[2,2048,128]{2,1,0:T(8,128)} %constant.2.clone.tab_hbm, bf16[4096,128]{1,0:T(8,128)(2,1)} %wq_hbm.1, ...), custom_call_target="tpu_custom_call" | custom-call | tf_op jit(solution)/shard_map/layer/pallas_call | solution.py:434
  131.9 6.2 %store.1 = (bf16[2048,4096]{1,0:T(8,128)(2,1)}, bf16[2048,128]{1,0:T(8,128)(2,1)}, bf16[2048,128]{1,0:T(8,128)(2,1)}) custom-call(bf16[2048,4096]{1,0:T(8,128)(2,1)S(1)} %get-tuple-element.9.y_ref, bf16[2048,128]{1,0:T(8,128)(2,1)S(1)} %get-tuple-element.10.k_ref, bf16[2048,128]{1,0:T(8,128)(2,1)S(1)} %get-tuple-element.11.v_ref), custom_call_target="tpu_custom_call" | custom-call | tf_op jit(solution)/shard_map/store/pallas_call | solution.py:470
